TPU v7x, 128 devices: a whole 4x4x4 slice. The times are simulated.
128 devices in a mesh: layer: 32 (over z, x, core), split: 4 (over y).
Axes of the slice: x: 4, y: 4, z: 4, core: 2. Of those that a mesh axis runs over, the one named last changes fastest.
Arguments:
- right_side: float32 [128, 512, 128], P('layer', 'split'), may hold values from -6 to 6
- diagonal: float32 [128, 512, 128], P('layer', 'split'), may hold values from 0.1 to 1
- inverses: float32 [128, 512, 512], P('layer', None, 'split'), may hold values from -1 to 1, as said below
Outputs:
- solution_field: float32 [128, 512, 128], P('layer', 'split')
- residual: float32 [128, 512, 128], P('layer', 'split')
Inputs may be any that keep to these rules, and one draw needn't show every extreme that they name: `inverses`: each plane's inverse is a diagonal matrix with entries between 0.5 and 1 plus a dense coupling with zero diagonal and spectral norm below 0.2.
All inputs are finite; a program needn't handle non-finite values.
Results may differ from a plain program's by a relative error of at most 0.0003.
Values sent between devices are 32-bit elements; how exact they have to be, the bound alone decides.
A program may use at most 64 MiB of HBM per device.

v0:
```python
import functools

import jax
import jax.numpy as jnp
from jax import lax
from jax.sharding import Mesh
from jax.sharding import PartitionSpec as P

LAYER_SPLIT = ("layer_0", "layer_1", "layer_2", "split")
LAYER = ("layer_0", "layer_1", "layer_2")


def extended(x, sides, width):
    edges = {}
    for axis, dim in sides:
        size, length = (lax.axis_size(axis), x.shape[dim])
        up = [(i, (i + 1) % size) for i in range(size - 1)]
        last = lax.slice_in_dim(x, length - width, length, axis=dim)
        first = lax.slice_in_dim(x, 0, width, axis=dim)
        edges[dim] = (
            lax.ppermute(last, axis, up),
            lax.ppermute(first, axis, [(b, a) for a, b in up]),
        )
    done = []
    for _, dim in sides:
        low, high = edges[dim]
        around = [(width, width) if d in done else (0, 0) for d in range(x.ndim)]
        x = jnp.concatenate([jnp.pad(low, around), x, jnp.pad(high, around)], axis=dim)
        done.append(dim)
    return x


def from_behind(block, axis, distance):
    devices = range(lax.axis_size(axis))
    route = [(i - distance, i) for i in devices if i - distance in devices]
    return lax.ppermute(block, axis, route)


def one_axis_at_a_time(x, axes):
    return functools.reduce(lax.psum, axes, x)


def stencil(values, diagonal):
    padded = extended(values, ((LAYER, 0), ("split", 1)), 1)
    beside = padded[2:, 1:-1, :] + padded[:-2, 1:-1, :]
    beside = beside + padded[1:-1, 2:, :] + padded[1:-1, :-2, :]
    centre_part = padded[1:-1, 1:-1, :]
    y_upper = jnp.pad(centre_part[:, :, 1:], ((0, 0), (0, 0), (0, 1)))
    y_lower = jnp.pad(centre_part[:, :, :-1], ((0, 0), (0, 0), (1, 0)))
    return (6.0 + diagonal) * values - beside - y_upper - y_lower


def down_local(matrices, portion, carried):

    def down_advance(state, inputs):
        matrix, source = inputs
        state = jnp.dot(matrix, source + state, precision=lax.Precision.HIGHEST)
        return (state, state)

    return lax.scan(down_advance, carried, (matrices, portion))


def up_local(matrices, portion, carried):

    def up_advance(state, inputs):
        matrix, below = inputs
        state = below + jnp.dot(matrix, state, precision=lax.Precision.HIGHEST)
        return (state, state)

    return lax.scan(up_advance, carried, (matrices, portion), reverse=True)


def chain_sweep(sweep_fn, matrices, source, sender, anchor, nblocks):
    depth_count = lax.axis_size(LAYER)
    block_width = source.shape[2] // nblocks
    plane_shape = (source.shape[1], block_width)
    result = jnp.zeros_like(source)
    incoming = jnp.zeros(plane_shape, jnp.float32)

    def chain_advance(turn, state):
        result, incoming = state
        block_raw = turn - anchor
        active = jnp.logical_and(block_raw >= 0, block_raw < nblocks)

        def working(unused):
            return sweep_fn(matrices, source, incoming)

        def resting(unused):
            return (jnp.zeros(plane_shape, jnp.float32), jnp.zeros_like(source))

        outgoing, stacked = lax.cond(active, working, resting, None)
        previous = result
        result = jnp.where(active, stacked, previous)
        return (result, sender(outgoing))

    result, incoming = lax.fori_loop(
        0, depth_count + nblocks - 1, chain_advance, (result, incoming)
    )
    return result


def per_device(right_side, diagonal, inverses):
    matrices = lax.all_gather(inverses, "split", axis=2, tiled=True)
    columns = lax.all_to_all(right_side, "split", split_axis=2, concat_axis=1, tiled=True)
    nblocks = 1
    own_index = lax.axis_index(LAYER)
    depth_count = lax.axis_size(LAYER)
    applied_rhs = stencil(right_side, diagonal)

    def send_down(values):
        return from_behind(values, LAYER, 1)

    def send_up(values):
        return from_behind(values, LAYER, -1)

    lower_sweep = chain_sweep(down_local, matrices, columns, send_down, own_index, nblocks)
    upper_sweep = chain_sweep(
        up_local, matrices, lower_sweep, send_up, depth_count - 1 - own_index, nblocks
    )
    direction = lax.all_to_all(upper_sweep, "split", split_axis=1, concat_axis=2, tiled=True)
    image = stencil(direction, diagonal)
    applied_image = stencil(image, diagonal)
    sums_all = (
        one_axis_at_a_time(jnp.sum(right_side * right_side), LAYER_SPLIT),
        one_axis_at_a_time(jnp.sum(right_side * image), LAYER_SPLIT),
        one_axis_at_a_time(jnp.sum(applied_rhs * right_side), LAYER_SPLIT),
        one_axis_at_a_time(jnp.sum(applied_rhs * image), LAYER_SPLIT),
        one_axis_at_a_time(jnp.sum(applied_image * right_side), LAYER_SPLIT),
        one_axis_at_a_time(jnp.sum(applied_image * image), LAYER_SPLIT),
        one_axis_at_a_time(jnp.sum(applied_rhs * applied_rhs), LAYER_SPLIT),
        one_axis_at_a_time(jnp.sum(applied_rhs * applied_image), LAYER_SPLIT),
        one_axis_at_a_time(jnp.sum(applied_image * applied_image), LAYER_SPLIT),
    )
    (
        norm_sq,
        curv_sum,
        rhs_rhs,
        rhs_image,
        image_rhs,
        image_image,
        arhs_arhs,
        arhs_aimage,
        aimage_aimage,
    ) = sums_all
    step_alpha = norm_sq / curv_sum
    middle = right_side - step_alpha * image
    tangent = applied_rhs - step_alpha * applied_image
    cross_sum = (
        rhs_rhs - step_alpha * (rhs_image + image_rhs) + step_alpha * step_alpha * image_image
    )
    self_sum = arhs_arhs - 2.0 * step_alpha * arhs_aimage + step_alpha * step_alpha * aimage_aimage
    step_omega = cross_sum / self_sum
    solution_field = step_alpha * direction + step_omega * middle
    residual = middle - step_omega * tangent
    return (solution_field, residual)


def solution(mesh):
    torus = Mesh(
        mesh.devices.reshape(4, 4, 2, mesh.shape["split"]),
        ("layer_0", "layer_1", "layer_2", "split"),
    )
    in_specs = (P(LAYER, "split", None), P(LAYER, "split", None), P(LAYER, None, "split"))
    out_specs = (P(LAYER, "split", None), P(LAYER, "split", None))
    return jax.shard_map(
        per_device, mesh=torus, in_specs=in_specs, out_specs=out_specs, check_vma=False
    )
```

profile of v0, /device:TPU:0, one launch (start us, length us, event | category | flops | bytes accessed | tf_op | source)
XLA Modules:
  0.0 1178.2 jit_solution(16858908235381505439)
XLA Ops:
  21.1 42.4 %all-gather.2.cloned.1.call-done = f32[4,512,512]{2,1,0:T(8,128)} async-done(((f32[4,512,128]{2,1,0:T(8,128)}), f32[4,512,512]{2,1,0:T(8,128)}) %all-gather.2.cloned.1.call-update) | async-done | bytes 4194320 | tf_op jit(solution)/shard_map/all_gather | solution.py:103
  63.5 331.8 %while.60 = (s32[]{:T(128)}, f32[4,512,32]{1,2,0:T(8,128)S(1)}, f32[512,32]{0,1:T(8,128)S(1)}, s32[]{:T(128)}, f32[4,512,512]{2,1,0:T(8,128)}, /*index=5*/f32[4,512,32]{1,2,0:T(8,128)S(1)}, s32[]{:T(128)}, s32[]{:T(128)}) while((s32[]{:T(128)}, f32[4,512,32]{1,2,0:T(8,128)S(1)}, f32[512,32]{0,1:T(8,128)S(1)}, s32[]{:T(128)}, ...), condition=%wide.region_10.11_spmd.clone, body=%wide.region_5.10_spmd.clone.sunk | while | flops 100810760 | bytes 2623315 | solution.py:96
  63.5 11.7 conditional.6
  63.5 11.7 while.58
  78.4 13.0 %collective-permute-start.1 = (f32[512,32]{0,1:T(8,128)S(1)}, f32[512,32]{0,1:T(8,128)S(1)}, u32[]{:S(2)}, u32[]{:S(2)}) collective-permute-start(f32[512,32]{0,1:T(8,128)S(1)} %get-tuple-element.667), channel_id=1, source_target_pairs={{0,4},{4,8},{8,12},{12,16},{16,20},{20,24},{24,28},{28,32},{32,36}... | collective-permute-start | bytes 196616 | tf_op jit(solution)/shard_map/while/body/eval_jaxpr/ppermute | solution.py:36
  97.0 15.7 %collective-permute-start.1 = (f32[512,32]{0,1:T(8,128)S(1)}, f32[512,32]{0,1:T(8,128)S(1)}, u32[]{:S(2)}, u32[]{:S(2)}) collective-permute-start(f32[512,32]{0,1:T(8,128)S(1)} %get-tuple-element.667), channel_id=1, source_target_pairs={{0,4},{4,8},{8,12},{12,16},{16,20},{20,24},{24,28},{28,32},{32,36}... | collective-permute-start | bytes 196616 | tf_op jit(solution)/shard_map/while/body/eval_jaxpr/ppermute | solution.py:36
  120.6 10.5 collective-permute-start.1
  139.0 13.3 %collective-permute-start.1 = (f32[512,32]{0,1:T(8,128)S(1)}, f32[512,32]{0,1:T(8,128)S(1)}, u32[]{:S(2)}, u32[]{:S(2)}) collective-permute-start(f32[512,32]{0,1:T(8,128)S(1)} %get-tuple-element.667), channel_id=1, source_target_pairs={{0,4},{4,8},{8,12},{12,16},{16,20},{20,24},{24,28},{28,32},{32,36}... | collective-permute-start | bytes 196616 | tf_op jit(solution)/shard_map/while/body/eval_jaxpr/ppermute | solution.py:36
  160.3 10.5 collective-permute-start.1
  178.6 13.3 %collective-permute-start.1 = (f32[512,32]{0,1:T(8,128)S(1)}, f32[512,32]{0,1:T(8,128)S(1)}, u32[]{:S(2)}, u32[]{:S(2)}) collective-permute-start(f32[512,32]{0,1:T(8,128)S(1)} %get-tuple-element.667), channel_id=1, source_target_pairs={{0,4},{4,8},{8,12},{12,16},{16,20},{20,24},{24,28},{28,32},{32,36}... | collective-permute-start | bytes 196616 | tf_op jit(solution)/shard_map/while/body/eval_jaxpr/ppermute | solution.py:36
  199.9 10.5 collective-permute-start.1
  218.3 15.4 %collective-permute-start.1 = (f32[512,32]{0,1:T(8,128)S(1)}, f32[512,32]{0,1:T(8,128)S(1)}, u32[]{:S(2)}, u32[]{:S(2)}) collective-permute-start(f32[512,32]{0,1:T(8,128)S(1)} %get-tuple-element.667), channel_id=1, source_target_pairs={{0,4},{4,8},{8,12},{12,16},{16,20},{20,24},{24,28},{28,32},{32,36}... | collective-permute-start | bytes 196616 | tf_op jit(solution)/shard_map/while/body/eval_jaxpr/ppermute | solution.py:36
  235.4 6.8 collective-permute-start.1
  243.8 8.3 collective-permute-start.1
  253.7 6.8 collective-permute-start.1
  262.2 11.2 collective-permute-start.1
  275.0 6.8 collective-permute-start.1
  283.4 8.3 collective-permute-start.1
  293.4 6.8 collective-permute-start.1
  301.8 11.2 collective-permute-start.1
  314.7 6.8 collective-permute-start.1
  323.1 8.3 collective-permute-start.1
  341.5 11.2 collective-permute-start.1
  362.7 8.3 collective-permute-start.1
  381.1 13.3 %collective-permute-start.1 = (f32[512,32]{0,1:T(8,128)S(1)}, f32[512,32]{0,1:T(8,128)S(1)}, u32[]{:S(2)}, u32[]{:S(2)}) collective-permute-start(f32[512,32]{0,1:T(8,128)S(1)} %get-tuple-element.667), channel_id=1, source_target_pairs={{0,4},{4,8},{8,12},{12,16},{16,20},{20,24},{24,28},{28,32},{32,36}... | collective-permute-start | bytes 196616 | tf_op jit(solution)/shard_map/while/body/eval_jaxpr/ppermute | solution.py:36
  395.3 686.7 %while.61 = (s32[]{:T(128)}, f32[4,512,32]{1,2,0:T(8,128)S(1)}, f32[512,32]{0,1:T(8,128)S(1)}, s32[]{:T(128)}, f32[4,512,32]{1,2,0:T(8,128)S(1)}, /*index=5*/f32[4,512,512]{2,1,0:T(8,128)}, s32[]{:T(128)}, s32[]{:T(128)}) while((s32[]{:T(128)}, f32[4,512,32]{1,2,0:T(8,128)S(1)}, f32[512,32]{0,1:T(8,128)S(1)}, s32[]{:T(128)}, ...), condition=%wide.region_16.17_spmd.clone, body=%wide.region_11.16_spmd.clone.sunk | while | flops 100810760 | bytes 2884979 | solution.py:96
  405.8 8.5 collective-permute-done
  424.6 11.3 collective-permute-done
  446.4 8.5 collective-permute-done
  465.2 11.3 collective-permute-done
  487.1 8.3 collective-permute-done
  506.0 11.2 collective-permute-done
  527.7 8.3 collective-permute-done
  546.6 13.3 %collective-permute-done = f32[512,32]{0,1:T(8,128)S(1)} collective-permute-done((f32[512,32]{0,1:T(8,128)S(1)}, f32[512,32]{0,1:T(8,128)S(1)}, u32[]{:S(2)}, u32[]{:S(2)}) %collective-permute-start) | collective-permute-done | bytes 65568 | tf_op jit(solution)/shard_map/while/body/eval_jaxpr/ppermute | solution.py:36
  570.4 8.3 collective-permute-done
  589.3 11.2 collective-permute-done
  611.1 8.3 collective-permute-done
  629.9 11.2 collective-permute-done
  651.7 8.3 collective-permute-done
  670.5 11.2 collective-permute-done
  692.3 8.3 collective-permute-done
  702.7 363.7 %collective-permute-done = f32[512,32]{0,1:T(8,128)S(1)} collective-permute-done((f32[512,32]{0,1:T(8,128)S(1)}, f32[512,32]{0,1:T(8,128)S(1)}, u32[]{:S(2)}, u32[]{:S(2)}) %collective-permute-start) | collective-permute-done | bytes 65568 | tf_op jit(solution)/shard_map/while/body/eval_jaxpr/ppermute | solution.py:36
  1066.4 12.4 %conditional.7 = (f32[512,32]{0,1:T(8,128)S(1)}, f32[4,512,32]{1,2,0:T(8,128)}) conditional(s32[]{:T(128)} %convert_element_type.34, () %tuple.153, (f32[4,512,32]{1,2,0:T(8,128)S(1)}, f32[4,512,512]{2,1,0:T(8,128)}, f32[512,32]{0,1:T(8,128)S(1)}) %tuple.154), branch_computations={%region_12.12_spmd, %region_13.15_spmd} | conditional | flops 100679680 | bytes 1836205 | solution.py:91
  1067.1 11.7 while.59
  1087.7 7.0 all-to-all-done.1
  1132.6 8.5 all-reduce.14
  1141.1 11.2 all-reduce.13
  1155.5 9.0 all-reduce.12
  (426 shorter events, 395.8 us)
Async XLA Ops:
  7.2 56.4 %all-gather.2.cloned.1.call-start = ((), (), s32[]{:S(2)}) async-start(), calls=%async_computation.2 | async-start | bytes 5242880 | tf_op jit(solution)/shard_map/all_gather | solution.py:103
  9.7 11.4 all-to-all-start
  16.0 1110.1 %collective-permute-start.6 = (f32[1,128,128]{1,2,0:T(8,128)}, f32[1,128,128]{1,2,0:T(8,128)S(1)}, u32[]{:S(2)}, u32[]{:S(2)}) collective-permute-start(f32[1,128,128]{1,2,0:T(8,128)} %get-tuple-element.529), channel_id=1, source_target_pairs={{4,0},{8,4},{12,8},{16,12},{20,16},{24,20},{28,24},{32,28},{36,32}... | collective-permute-start | bytes 196616 | tf_op jit(solution)/shard_map/ppermute | solution.py:22
  78.4 13.9 %collective-permute-start.1 = (f32[512,32]{0,1:T(8,128)S(1)}, f32[512,32]{0,1:T(8,128)S(1)}, u32[]{:S(2)}, u32[]{:S(2)}) collective-permute-start(f32[512,32]{0,1:T(8,128)S(1)} %get-tuple-element.667), channel_id=1, source_target_pairs={{0,4},{4,8},{8,12},{12,16},{16,20},{20,24},{24,28},{28,32},{32,36}... | collective-permute-start | bytes 196616 | tf_op jit(solution)/shard_map/while/body/eval_jaxpr/ppermute | solution.py:36
  97.0 16.6 %collective-permute-start.1 = (f32[512,32]{0,1:T(8,128)S(1)}, f32[512,32]{0,1:T(8,128)S(1)}, u32[]{:S(2)}, u32[]{:S(2)}) collective-permute-start(f32[512,32]{0,1:T(8,128)S(1)} %get-tuple-element.667), channel_id=1, source_target_pairs={{0,4},{4,8},{8,12},{12,16},{16,20},{20,24},{24,28},{28,32},{32,36}... | collective-permute-start | bytes 196616 | tf_op jit(solution)/shard_map/while/body/eval_jaxpr/ppermute | solution.py:36
  120.6 11.3 collective-permute-start.1
  139.0 14.2 %collective-permute-start.1 = (f32[512,32]{0,1:T(8,128)S(1)}, f32[512,32]{0,1:T(8,128)S(1)}, u32[]{:S(2)}, u32[]{:S(2)}) collective-permute-start(f32[512,32]{0,1:T(8,128)S(1)} %get-tuple-element.667), channel_id=1, source_target_pairs={{0,4},{4,8},{8,12},{12,16},{16,20},{20,24},{24,28},{28,32},{32,36}... | collective-permute-start | bytes 196616 | tf_op jit(solution)/shard_map/while/body/eval_jaxpr/ppermute | solution.py:36
  160.3 11.3 collective-permute-start.1
  178.6 14.2 %collective-permute-start.1 = (f32[512,32]{0,1:T(8,128)S(1)}, f32[512,32]{0,1:T(8,128)S(1)}, u32[]{:S(2)}, u32[]{:S(2)}) collective-permute-start(f32[512,32]{0,1:T(8,128)S(1)} %get-tuple-element.667), channel_id=1, source_target_pairs={{0,4},{4,8},{8,12},{12,16},{16,20},{20,24},{24,28},{28,32},{32,36}... | collective-permute-start | bytes 196616 | tf_op jit(solution)/shard_map/while/body/eval_jaxpr/ppermute | solution.py:36
  199.9 11.3 collective-permute-start.1
  218.3 16.3 %collective-permute-start.1 = (f32[512,32]{0,1:T(8,128)S(1)}, f32[512,32]{0,1:T(8,128)S(1)}, u32[]{:S(2)}, u32[]{:S(2)}) collective-permute-start(f32[512,32]{0,1:T(8,128)S(1)} %get-tuple-element.667), channel_id=1, source_target_pairs={{0,4},{4,8},{8,12},{12,16},{16,20},{20,24},{24,28},{28,32},{32,36}... | collective-permute-start | bytes 196616 | tf_op jit(solution)/shard_map/while/body/eval_jaxpr/ppermute | solution.py:36
  235.4 7.7 collective-permute-start.1
  243.8 9.2 collective-permute-start.1
  253.7 7.7 collective-permute-start.1
  262.2 12.1 %collective-permute-start.1 = (f32[512,32]{0,1:T(8,128)S(1)}, f32[512,32]{0,1:T(8,128)S(1)}, u32[]{:S(2)}, u32[]{:S(2)}) collective-permute-start(f32[512,32]{0,1:T(8,128)S(1)} %get-tuple-element.667), channel_id=1, source_target_pairs={{0,4},{4,8},{8,12},{12,16},{16,20},{20,24},{24,28},{28,32},{32,36}... | collective-permute-start | bytes 196616 | tf_op jit(solution)/shard_map/while/body/eval_jaxpr/ppermute | solution.py:36
  275.0 7.7 collective-permute-start.1
  283.4 9.2 collective-permute-start.1
  293.4 7.7 collective-permute-start.1
  301.8 12.1 %collective-permute-start.1 = (f32[512,32]{0,1:T(8,128)S(1)}, f32[512,32]{0,1:T(8,128)S(1)}, u32[]{:S(2)}, u32[]{:S(2)}) collective-permute-start(f32[512,32]{0,1:T(8,128)S(1)} %get-tuple-element.667), channel_id=1, source_target_pairs={{0,4},{4,8},{8,12},{12,16},{16,20},{20,24},{24,28},{28,32},{32,36}... | collective-permute-start | bytes 196616 | tf_op jit(solution)/shard_map/while/body/eval_jaxpr/ppermute | solution.py:36
  323.1 9.2 collective-permute-start.1
  341.5 12.1 %collective-permute-start.1 = (f32[512,32]{0,1:T(8,128)S(1)}, f32[512,32]{0,1:T(8,128)S(1)}, u32[]{:S(2)}, u32[]{:S(2)}) collective-permute-start(f32[512,32]{0,1:T(8,128)S(1)} %get-tuple-element.667), channel_id=1, source_target_pairs={{0,4},{4,8},{8,12},{12,16},{16,20},{20,24},{24,28},{28,32},{32,36}... | collective-permute-start | bytes 196616 | tf_op jit(solution)/shard_map/while/body/eval_jaxpr/ppermute | solution.py:36
  362.7 9.2 collective-permute-start.1
  381.1 14.2 %collective-permute-start.1 = (f32[512,32]{0,1:T(8,128)S(1)}, f32[512,32]{0,1:T(8,128)S(1)}, u32[]{:S(2)}, u32[]{:S(2)}) collective-permute-start(f32[512,32]{0,1:T(8,128)S(1)} %get-tuple-element.667), channel_id=1, source_target_pairs={{0,4},{4,8},{8,12},{12,16},{16,20},{20,24},{24,28},{28,32},{32,36}... | collective-permute-start | bytes 196616 | tf_op jit(solution)/shard_map/while/body/eval_jaxpr/ppermute | solution.py:36
  404.4 9.9 collective-permute-start
  423.2 12.7 %collective-permute-start = (f32[512,32]{0,1:T(8,128)S(1)}, f32[512,32]{0,1:T(8,128)S(1)}, u32[]{:S(2)}, u32[]{:S(2)}) collective-permute-start(f32[512,32]{0,1:T(8,128)S(1)} %get-tuple-element.675), channel_id=1, source_target_pairs={{4,0},{8,4},{12,8},{16,12},{20,16},{24,20},{28,24},{32,28},{36,32}... | collective-permute-start | bytes 196616 | tf_op jit(solution)/shard_map/while/body/eval_jaxpr/ppermute | solution.py:36
  445.0 9.9 collective-permute-start
  463.8 12.7 %collective-permute-start = (f32[512,32]{0,1:T(8,128)S(1)}, f32[512,32]{0,1:T(8,128)S(1)}, u32[]{:S(2)}, u32[]{:S(2)}) collective-permute-start(f32[512,32]{0,1:T(8,128)S(1)} %get-tuple-element.675), channel_id=1, source_target_pairs={{4,0},{8,4},{12,8},{16,12},{20,16},{24,20},{28,24},{32,28},{36,32}... | collective-permute-start | bytes 196616 | tf_op jit(solution)/shard_map/while/body/eval_jaxpr/ppermute | solution.py:36
  485.7 9.7 collective-permute-start
  504.6 12.6 %collective-permute-start = (f32[512,32]{0,1:T(8,128)S(1)}, f32[512,32]{0,1:T(8,128)S(1)}, u32[]{:S(2)}, u32[]{:S(2)}) collective-permute-start(f32[512,32]{0,1:T(8,128)S(1)} %get-tuple-element.675), channel_id=1, source_target_pairs={{4,0},{8,4},{12,8},{16,12},{20,16},{24,20},{28,24},{32,28},{36,32}... | collective-permute-start | bytes 196616 | tf_op jit(solution)/shard_map/while/body/eval_jaxpr/ppermute | solution.py:36
  526.3 9.7 collective-permute-start
  545.2 14.7 %collective-permute-start = (f32[512,32]{0,1:T(8,128)S(1)}, f32[512,32]{0,1:T(8,128)S(1)}, u32[]{:S(2)}, u32[]{:S(2)}) collective-permute-start(f32[512,32]{0,1:T(8,128)S(1)} %get-tuple-element.675), channel_id=1, source_target_pairs={{4,0},{8,4},{12,8},{16,12},{20,16},{24,20},{28,24},{32,28},{36,32}... | collective-permute-start | bytes 196616 | tf_op jit(solution)/shard_map/while/body/eval_jaxpr/ppermute | solution.py:36
  569.0 9.7 collective-permute-start
  587.9 12.6 %collective-permute-start = (f32[512,32]{0,1:T(8,128)S(1)}, f32[512,32]{0,1:T(8,128)S(1)}, u32[]{:S(2)}, u32[]{:S(2)}) collective-permute-start(f32[512,32]{0,1:T(8,128)S(1)} %get-tuple-element.675), channel_id=1, source_target_pairs={{4,0},{8,4},{12,8},{16,12},{20,16},{24,20},{28,24},{32,28},{36,32}... | collective-permute-start | bytes 196616 | tf_op jit(solution)/shard_map/while/body/eval_jaxpr/ppermute | solution.py:36
  609.7 9.7 collective-permute-start
  628.5 12.6 %collective-permute-start = (f32[512,32]{0,1:T(8,128)S(1)}, f32[512,32]{0,1:T(8,128)S(1)}, u32[]{:S(2)}, u32[]{:S(2)}) collective-permute-start(f32[512,32]{0,1:T(8,128)S(1)} %get-tuple-element.675), channel_id=1, source_target_pairs={{4,0},{8,4},{12,8},{16,12},{20,16},{24,20},{28,24},{32,28},{36,32}... | collective-permute-start | bytes 196616 | tf_op jit(solution)/shard_map/while/body/eval_jaxpr/ppermute | solution.py:36
  650.3 9.7 collective-permute-start
  669.1 12.6 %collective-permute-start = (f32[512,32]{0,1:T(8,128)S(1)}, f32[512,32]{0,1:T(8,128)S(1)}, u32[]{:S(2)}, u32[]{:S(2)}) collective-permute-start(f32[512,32]{0,1:T(8,128)S(1)} %get-tuple-element.675), channel_id=1, source_target_pairs={{4,0},{8,4},{12,8},{16,12},{20,16},{24,20},{28,24},{32,28},{36,32}... | collective-permute-start | bytes 196616 | tf_op jit(solution)/shard_map/while/body/eval_jaxpr/ppermute | solution.py:36
  690.9 9.7 collective-permute-start
  701.3 365.1 %collective-permute-start = (f32[512,32]{0,1:T(8,128)S(1)}, f32[512,32]{0,1:T(8,128)S(1)}, u32[]{:S(2)}, u32[]{:S(2)}) collective-permute-start(f32[512,32]{0,1:T(8,128)S(1)} %get-tuple-element.675), channel_id=1, source_target_pairs={{4,0},{8,4},{12,8},{16,12},{20,16},{24,20},{28,24},{32,28},{36,32}... | collective-permute-start | bytes 196616 | tf_op jit(solution)/shard_map/while/body/eval_jaxpr/ppermute | solution.py:36
  1083.8 10.9 all-to-all-start.1
  1098.3 11.3 collective-permute-start.4
  1099.6 12.0 %collective-permute-start.5 = (f32[4,1,128]{1,2,0:T(8,128)}, f32[4,1,128]{1,2,0:T(8,128)}, u32[]{:S(2)}, u32[]{:S(2)}) collective-permute-start(f32[4,1,128]{1,2,0:T(8,128)} %get-tuple-element.535), channel_id=1, source_target_pairs={{0,1},{1,2},{2,3},{4,5},{5,6},{6,7},{8,9},{9,10},{10,11},{12,13},{... | collective-permute-start | bytes 6152 | tf_op jit(solution)/shard_map/ppermute | solution.py:21
  1106.6 10.9 collective-permute-start.3
  1109.7 19.5 %collective-permute-start.7 = (f32[1,128,128]{1,2,0:T(8,128)S(1)}, f32[1,128,128]{1,2,0:T(8,128)S(1)}, u32[]{:S(2)}, u32[]{:S(2)}) collective-permute-start(f32[1,128,128]{1,2,0:T(8,128)S(1)} %get-tuple-element.528), channel_id=1, source_target_pairs={{0,4},{4,8},{8,12},{12,16},{16,20},{20,24},{24,28},{28,32},{32,36}... | collective-permute-start | bytes 196616 | tf_op jit(solution)/shard_map/ppermute | solution.py:21
  1111.6 10.1 collective-permute-start.8
  1112.9 11.9 %collective-permute-start.9 = (f32[4,1,128]{1,2,0:T(8,128)S(1)}, f32[4,1,128]{1,2,0:T(8,128)S(1)}, u32[]{:S(2)}, u32[]{:S(2)}) collective-permute-start(f32[4,1,128]{1,2,0:T(8,128)S(1)} %copy.64), channel_id=1, source_target_pairs={{0,1},{1,2},{2,3},{4,5},{5,6},{6,7},{8,9},{9,10},{10,11},{12,13},{... | collective-permute-start | bytes 6152 | tf_op jit(solution)/shard_map/ppermute | solution.py:21
  1118.9 10.3 collective-permute-start.12
  1121.7 7.9 collective-permute-start.13
  (31 other events, 204.0 us)
Sparse Core Ops, SparseCore 0:
  9.6 53.8 all-gather.1
where the time goes:
time: 1180 us
  waiting for transfers between devices  682 us (58%)
  starting transfers between devices  347 us (29%)
  local copies, waits for them, and re-layouts  58.4 us (5%)
  blocking collectives  31.9 us (3%)
  matrix products  23.3 us (2%)
  between operations  20.7 us (2%)
  other arithmetic  13.6 us (1%)
    ppermute x64, waiting for transfers between devices, from_behind(): return lax.ppermute(block, axis, route)  629 us
    ppermute x64, starting transfers between devices, from_behind(): return lax.ppermute(block, axis, route)  310 us
    another operation x127, local copies, waits for them, and re-layouts  46.3 us
    all_gather x1, waiting for transfers between devices, per_device(): matrices = lax.all_gather(inverses, 'split', axis=2, tiled=True)  42.4 us
    psum x4, blocking collectives, one_axis_at_a_time(): return functools.reduce(lax.psum, axes, x)  31.9 us
  transfers between devices with their start and end apart: 79, of which 68 were waited for; matrix products, arithmetic and copies ran while one was open for 8% of the time, Pallas kernels for 0%

commit v1 on v0

v1 whole, which is shorter than its diff:
```python
import functools

import jax
import jax.numpy as jnp
from jax import lax
from jax.experimental import pallas as pl
from jax.experimental.pallas import tpu as pltpu
from jax.sharding import PartitionSpec as P

MESH = pl.DeviceIdType.MESH
F32 = jnp.float32
BF16 = jnp.bfloat16


def split2(x):
    high = x.astype(BF16)
    return high, (x - high.astype(F32)).astype(BF16)


def mm(x, w_high, w_low):
    high, low = split2(x)
    dot = functools.partial(jnp.dot, preferred_element_type=F32)
    return dot(high, w_high) + (dot(low, w_high) + dot(high, w_low))


def mm_ref(x, pair):
    return mm(x, pair[0], pair[1])


def store_pair(pair, x):
    high, low = split2(x)
    pair[0] = high
    pair[1] = low


def sweep_kernel(
    nlayer, nsplit, nchunk,
    rhs_ref, inv_ref, out_ref,
    gbuf, mats, rsend, cols, low, pf, qf, pown, qown, pall, qall, pin, qin,
    cvec, cin, ain, aout, amid, evec, ein, bin_, bout, bcore,
    rs_send, rs_recv, g_send, g_recv, c_send, c_recv, d_send, d_recv, u_send, u_recv,
):
    planes, nx, width = inv_ref.shape
    ysize = rhs_ref.shape[2]
    yb = ysize // nsplit
    cb = yb // nchunk
    half = width // 2
    layer = lax.axis_index("layer")
    s = lax.axis_index("split")
    core = lax.rem(layer, 2)
    chip = layer // 2
    nchip = nlayer // 2
    right = lax.rem(s + 1, nsplit)
    left = lax.rem(s + nsplit - 1, nsplit)
    other = layer + 1 - 2 * core
    first = chip == 0
    last = chip == nchip - 1

    def rows(owner, start, size):
        return pl.ds(pl.multiple_of(owner * width + start, half), size)

    barrier = pltpu.get_barrier_semaphore()

    def greet(l, t):
        pl.semaphore_signal(barrier, inc=1, device_id=(l, t), device_id_type=MESH)

    for d in range(1, nsplit):
        greet(layer, lax.rem(s + d, nsplit))
    greet(other, s)

    @pl.when(jnp.logical_and(core == 0, jnp.logical_not(first)))
    def _():
        greet(layer - 2, s)

    @pl.when(jnp.logical_and(core == 0, jnp.logical_not(last)))
    def _():
        greet(layer + 2, s)

    for k in range(planes):
        gbuf[k, rows(s, 0, width), :] = inv_ref[k].T
    for k in range(planes):
        rsend[k] = rhs_ref[k].T
    for k in range(planes):
        cols[k, :, pl.ds(pl.multiple_of(s * width, width), width)] = rsend[
            k, pl.ds(pl.multiple_of(s * yb, yb), yb), :
        ]

    ends = jnp.where(first, 1, 0) + jnp.where(last, 1, 0)
    pl.semaphore_wait(barrier, nsplit + jnp.where(core == 0, 2 - ends, 0))

    def remote(src, dst, send, recv, l, t):
        return pltpu.make_async_remote_copy(
            src_ref=src, dst_ref=dst, send_sem=send, recv_sem=recv,
            device_id=(l, t), device_id_type=MESH,
        )

    def regroup(d):
        t = lax.rem(s + d, nsplit)
        return remote(
            rsend.at[:, pl.ds(pl.multiple_of(t * yb, yb), yb), :],
            cols.at[:, :, pl.ds(pl.multiple_of(s * width, width), width)],
            rs_send.at[d - 1], rs_recv.at[d - 1], layer, t,
        )

    def own_right(k):
        part = gbuf.at[k, rows(s, 0, width), :]
        return remote(part, part, g_send.at[0, k], g_recv.at[0, k], layer, right)

    def own_left(k):
        part = gbuf.at[k, rows(s, 0, width), :]
        return remote(part, part, g_send.at[1, k], g_recv.at[1, k], layer, left)

    def pass_right(k):
        part = gbuf.at[k, rows(left, 0, half), :]
        return remote(part, part, g_send.at[2, k], g_recv.at[2, k], layer, right)

    def pass_left(k):
        part = gbuf.at[k, rows(right, half, half), :]
        return remote(part, part, g_send.at[3, k], g_recv.at[3, k], layer, left)

    for d in range(1, nsplit):
        regroup(d).start()
    for k in range(min(2, planes)):
        own_right(k).start()
        own_left(k).start()

    def relay(k):
        own_right(k).wait_recv()
        pass_right(k).start()
        own_left(k).wait_recv()
        pass_left(k).start()
        if k + 2 < planes:
            own_right(k + 2).start()
            own_left(k + 2).start()

    def absorb(k):
        pass_right(k).wait_recv()
        pass_left(k).wait_recv()
        full = gbuf[k]
        high, lowpart = split2(full)
        mats[k, 0] = high
        mats[k, 1] = lowpart
        if k == 0:
            for d in range(1, nsplit):
                regroup(d).wait_recv()
            cvec[...] = mm(cols[0], high, lowpart)
            pf[...] = full
            qown[0] = high
            qown[1] = lowpart
        else:
            cvec[...] = mm(cols[k] + cvec[...], high, lowpart)
            pf[...] = mm(pf[...], high, lowpart)

    def absorb_up(k):
        if k > 0:
            qf[...] = mm(gbuf[k], qown[0], qown[1])
            store_pair(qown, qf[...])

    for k in range(planes):
        relay(k)
        if k > 0:
            absorb(k - 1)
            absorb_up(k - 1)
    absorb(planes - 1)

    give_p = remote(pf, pin, c_send.at[0], c_recv.at[0], other, s)
    give_q = remote(qf, qin, c_send.at[1], c_recv.at[1], other, s)
    give_c = remote(cvec, cin, c_send.at[2], c_recv.at[2], other, s)
    give_a = remote(amid, ain.at[pl.ds(0, yb), :], c_send.at[3], c_recv.at[3], other, s)
    give_e = remote(evec, ein, c_send.at[4], c_recv.at[4], other, s)

    def chunk(q):
        return pl.ds(q * cb, cb)

    def give_b(q):
        return remote(
            bin_.at[chunk(q), :], bcore.at[chunk(q), :],
            c_send.at[5 + q], c_recv.at[5 + q], other, s,
        )

    def hand_down(q):
        return remote(
            aout.at[chunk(q), :], ain.at[chunk(q), :], d_send.at[q], d_recv.at[q], layer + 2, s
        )

    def hand_up(q):
        return remote(
            bout.at[chunk(q), :], bin_.at[chunk(q), :], u_send.at[q], u_recv.at[q], layer - 2, s
        )

    @pl.when(core == 1)
    def _():
        give_c.start()
        give_p.start()

    absorb_up(planes - 1)

    def down_sweep(state):
        for k in range(planes):
            source = cols[k] if state is None else cols[k] + state
            state = mm(source, mats[k, 0], mats[k, 1])
            low[k] = state

    def up_partial():
        state = low[planes - 1]
        for k in range(planes - 2, -1, -1):
            state = low[k] + mm(state, mats[k, 0], mats[k, 1])
        evec[...] = state

    def up_sweep(state):
        for k in range(planes - 1, -1, -1):
            if state is None:
                state = low[k]
            else:
                state = low[k] + mm(state, mats[k, 0], mats[k, 1])
            out_ref[k] = state

    @pl.when(core == 1)
    def _():
        give_q.start()
        give_a.wait_recv()
        down_sweep(ain[pl.ds(0, yb), :])
        up_partial()
        give_e.start()

        @pl.when(last)
        def _():
            up_sweep(None)

        @pl.when(jnp.logical_not(last))
        def _():
            for q in range(nchunk):
                give_b(q).wait_recv()
            up_sweep(bcore[...])

        give_c.wait_send()
        give_p.wait_send()
        give_q.wait_send()
        give_e.wait_send()

    @pl.when(core == 0)
    def _():
        store_pair(pown, pf[...])
        give_c.wait_recv()
        give_p.wait_recv()
        store_pair(pin_pair := pall, pin[...])
        aout[...] = mm_ref(cvec[...], pin_pair) + cin[...]

        @pl.when(first)
        def _():
            for q in range(nchunk):
                hand_down(q).start()
            amid[...] = cvec[...]
            give_a.start()
            down_sweep(None)

        @pl.when(jnp.logical_not(first))
        def _():
            product = mm_ref(pf[...], pin_pair)
            store_pair(pall, product)
            for q in range(nchunk):
                hand_down(q).wait_recv()
                aout[chunk(q), :] = aout[chunk(q), :] + mm_ref(ain[chunk(q), :], pall)

                @pl.when(jnp.logical_not(last))
                def _():
                    hand_down(q).start()

            amid[...] = cvec[...] + mm_ref(ain[pl.ds(0, yb), :], pown)
            give_a.start()
            down_sweep(ain[pl.ds(0, yb), :])

        up_partial()
        give_q.wait_recv()
        store_pair(qin_pair := pown, qin[...])
        give_e.wait_recv()
        bout[...] = evec[...] + mm_ref(ein[...], qown)

        @pl.when(last)
        def _():
            for q in range(nchunk):
                hand_up(q).start()
            up_sweep(ein[...])

        @pl.when(jnp.logical_not(last))
        def _():
            store_pair(qall, mm_ref(qin[...], qown))
            for q in range(nchunk):
                hand_up(q).wait_recv()
                give_b(q).start()

                @pl.when(jnp.logical_not(first))
                def _():
                    bout[chunk(q), :] = bout[chunk(q), :] + mm_ref(bin_[chunk(q), :], qall)
                    hand_up(q).start()

            up_sweep(ein[...] + mm_ref(bin_[...], qin_pair))
            for q in range(nchunk):
                give_b(q).wait_send()
                hand_down(q).wait_send()

        @pl.when(jnp.logical_not(first))
        def _():
            for q in range(nchunk):
                hand_up(q).wait_send()

        give_a.wait_send()

    for d in range(1, nsplit):
        regroup(d).wait_send()
    for k in range(planes):
        own_right(k).wait_send()
        own_left(k).wait_send()
        pass_right(k).wait_send()
        pass_left(k).wait_send()


def sweeps(right_side, inverses, nlayer, nsplit):
    planes, nx, width = inverses.shape
    ysize = right_side.shape[2]
    yb = ysize // nsplit
    nchunk = 2
    vmem = pl.BlockSpec(memory_space=pltpu.VMEM)
    square = pltpu.VMEM((nx, nx), F32)
    pair = pltpu.VMEM((2, nx, nx), BF16)
    strip = pltpu.VMEM((yb, nx), F32)
    dma = pltpu.SemaphoreType.DMA
    return pl.pallas_call(
        functools.partial(sweep_kernel, nlayer, nsplit, nchunk),
        out_shape=jax.ShapeDtypeStruct((planes, yb, nx), F32),
        in_specs=[vmem, vmem],
        out_specs=vmem,
        scratch_shapes=[
            pltpu.VMEM((planes, nx, nx), F32),
            pltpu.VMEM((planes, 2, nx, nx), BF16),
            pltpu.VMEM((planes, ysize, width), F32),
            pltpu.VMEM((planes, yb, nx), F32),
            pltpu.VMEM((planes, yb, nx), F32),
            square, square, pair, pair, pair, pair, square, square,
            strip, strip, strip, strip, strip, strip, strip, strip, strip, strip,
            dma((nsplit - 1,)), dma((nsplit - 1,)),
            dma((4, planes)), dma((4, planes)),
            dma((5 + nchunk,)), dma((5 + nchunk,)),
            dma((nchunk,)), dma((nchunk,)),
            dma((nchunk,)), dma((nchunk,)),
        ],
        compiler_params=pltpu.CompilerParams(
            collective_id=0, has_side_effects=True, vmem_limit_bytes=56 * 1024 * 1024
        ),
        name="sweeps",
    )(right_side, inverses)


def shifted(x, axis, dim):
    size, length = lax.axis_size(axis), x.shape[dim]
    up = [(i, i + 1) for i in range(size - 1)]
    last = lax.slice_in_dim(x, length - 1, length, axis=dim)
    first = lax.slice_in_dim(x, 0, 1, axis=dim)
    low = lax.ppermute(last, axis, up)
    high = lax.ppermute(first, axis, [(b, a) for a, b in up])
    return low, high


def stencil(values, diagonal):
    low0, high0 = shifted(values, "layer", 0)
    low1, high1 = shifted(values, "split", 1)
    beside = jnp.concatenate([low0, values[:-1]], 0) + jnp.concatenate([values[1:], high0], 0)
    beside = beside + jnp.concatenate([low1, values[:, :-1]], 1)
    beside = beside + jnp.concatenate([values[:, 1:], high1], 1)
    y_upper = jnp.pad(values[:, :, 1:], ((0, 0), (0, 0), (0, 1)))
    y_lower = jnp.pad(values[:, :, :-1], ((0, 0), (0, 0), (1, 0)))
    return (6.0 + diagonal) * values - beside - y_upper - y_lower


def per_device(nlayer, nsplit, right_side, diagonal, inverses):
    applied_rhs = stencil(right_side, diagonal)
    swept = sweeps(right_side, inverses, nlayer, nsplit)
    regrouped = lax.all_to_all(swept, "split", split_axis=2, concat_axis=1, tiled=True)
    direction = jnp.swapaxes(regrouped, 1, 2)
    image = stencil(direction, diagonal)
    applied_image = stencil(image, diagonal)
    pairs = (
        (right_side, right_side), (right_side, image),
        (applied_rhs, right_side), (applied_rhs, image),
        (applied_image, right_side), (applied_image, image),
        (applied_rhs, applied_rhs), (applied_rhs, applied_image), (applied_image, applied_image),
    )
    sums = lax.psum(jnp.stack([jnp.sum(a * b) for a, b in pairs]), ("layer", "split"))
    rr, ri, ar, ai, br, bi, aa, ab, bb = [sums[i] for i in range(9)]
    alpha = rr / ri
    middle = right_side - alpha * image
    tangent = applied_rhs - alpha * applied_image
    cross = ar - alpha * (ai + br) + alpha * alpha * bi
    own = aa - 2.0 * alpha * ab + alpha * alpha * bb
    omega = cross / own
    return alpha * direction + omega * middle, middle - omega * tangent


def solution(mesh):
    spec = P("layer", "split", None)
    return jax.shard_map(
        functools.partial(per_device, mesh.shape["layer"], mesh.shape["split"]),
        mesh=mesh,
        in_specs=(spec, spec, P("layer", None, "split")),
        out_specs=(spec, spec),
        check_vma=False,
    )
```

time: 1180 us -> 294 us (0.25)
  waiting for transfers between devices: 682 us -> 9.8 us
  starting transfers between devices: 347 us -> 31.1 us
  Pallas kernels: 0 us -> 158 us
  local copies, waits for them, and re-layouts: 58.4 us -> 16 us
  blocking collectives: 31.9 us -> 67 us
  matrix products: 23.3 us -> 0 us
  between operations: 20.7 us -> 6.79 us
    ppermute x76 -> x12, waiting for transfers between devices: 632 us -> 7.06 us  [the longest x6 6.77 us: shifted(): low = lax.ppermute(last, axis, up)]
    ppermute x76 -> x12, starting transfers between devices: 338 us -> 27.5 us  [the longest x6 19.6 us: shifted(): low = lax.ppermute(last, axis, up)]
    pallas_call x0 -> x1, Pallas kernels: none -> 158 us  [sweeps(): pl.pallas_call(functools.partial(sweep_kernel, nlayer, nsplit, nchunk), o...]
    all_gather x1 -> x0, waiting for transfers between devices: 42.4 us -> none  [per_device(): matrices = lax.all_gather(inverses, 'split', axis=2, tiled=True)]
    another operation x127 -> x1, local copies, waits for them, and re-layouts: 46.3 us -> 5.73 us  [per_device(): jnp.stack([jnp.sum(a * b) for a, b in pairs])]
    psum x4 -> x1, blocking collectives: 31.9 us -> 67 us  [per_device(): lax.psum(jnp.stack([jnp.sum(a * b) for a, b in pairs]), ('layer', 'split'))]
    dot_general x8 -> x0, matrix products: 23.3 us -> none  [the longest x4 11.7 us: down_advance(): state = jnp.dot(matrix, source + state, precision=lax.Precision.HIGHEST)]
  transfers between devices with their start and end apart: 79 -> 13, of which waited for: 68 -> 5; matrix products, arithmetic and copies ran while one was open for 8% -> 2% of each run, Pallas kernels for 0% -> 0%
where the time goes in v1:
time: 294 us; the launch traced here: 293 us
  Pallas kernels  158 us (54%)
  blocking collectives  67 us (23%)
  starting transfers between devices  31.1 us (11%)
  local copies, waits for them, and re-layouts  16 us (5%)
  waiting for transfers between devices  9.8 us (3%)
  between operations  6.79 us (2%)
  other arithmetic  4.68 us (2%)
    pallas_call x1, Pallas kernels, sweeps(): pl.pallas_call(functools.partial(sweep_kernel, nlayer, nsplit, nchunk), o...  158 us
    psum x1, blocking collectives, per_device(): lax.psum(jnp.stack([jnp.sum(a * b) for a, b in pairs]), ('layer', 'split'))  67 us
    ppermute x6, starting transfers between devices, shifted(): low = lax.ppermute(last, axis, up)  19.6 us
    ppermute x6, starting transfers between devices, shifted(): high = lax.ppermute(first, axis, [(b, a) for a, b in up])  7.86 us
    ppermute x6, waiting for transfers between devices, shifted(): low = lax.ppermute(last, axis, up)  6.77 us
  transfers between devices with their start and end apart: 13, of which 5 were waited for; matrix products, arithmetic and copies ran while one was open for 2% of the time, Pallas kernels for 0%

profile of v1, /device:TPU:0, one launch (start us, length us, event | category | flops | bytes accessed | tf_op | source)
XLA Modules:
  0.0 293.0 jit_solution(12437456672038613255)
XLA Ops:
  0.6 157.6 %sweeps.1 = f32[4,32,512]{2,1,0:T(8,128)} custom-call(f32[4,128,128]{2,1,0:T(8,128)} %rhs_ref.1, f32[4,512,128]{2,1,0:T(8,128)} %inv_ref.1), custom_call_target="tpu_custom_call" | custom-call | tf_op jit(solution)/shard_map/sweeps/pallas_call | solution.py:328
  158.3 1.3 copy.45
  159.6 1.4 reshape.6
  161.0 3.6 %all-to-all-start = ((f32[4,1,16384]{2,1,0:T(1,128)}), f32[4,1,16384]{2,1,0:T(1,128)S(1)}, u32[]{:S(2)}, u32[]{:S(2)}) async-start(f32[4,1,16384]{2,1,0:T(1,128)} %reshape.6), calls=%async_computation | async-start | bytes 524288 | tf_op jit(solution)/shard_map/all_to_all | solution.py:378
  164.6 0.9 copy.57
  165.5 1.3 collective-permute-start.7
  166.8 0.1 copy.48
  167.0 0.1 fusion.25
  167.1 0.0 copy-start.1
  167.1 0.7 multiply_reduce_fusion.8
  167.8 0.3 copy-done.1
  168.1 0.1 copy.44
  168.2 0.9 copy.54
  169.1 0.7 fusion.22
  169.7 2.7 all-to-all-done
  172.5 0.5 broadcast.21
  173.0 1.4 reduce
  174.4 0.6 reshape.7
  174.9 0.3 copy.47
  175.3 0.1 fusion.28
  175.4 0.1 fusion.29
  175.6 1.8 collective-permute-start
  177.4 1.3 collective-permute-start.1
  178.7 2.5 collective-permute-start.2
  181.2 1.4 collective-permute-start.3
  182.7 5.0 %collective-permute-done.2 = f32[4,1,128]{1,2,0:T(8,128)S(1)} collective-permute-done((f32[4,1,128]{1,2,0:T(8,128)S(1)}, f32[4,1,128]{1,2,0:T(8,128)S(1)}, u32[]{:S(2)}, u32[]{:S(2)}) %collective-permute-start.2) | collective-permute-done | bytes 2080 | tf_op jit(solution)/shard_map/ppermute | solution.py:359
  187.7 4.4 %collective-permute-start.6 = (f32[4,1,128]{1,2,0:T(8,128)S(1)}, f32[4,1,128]{1,2,0:T(8,128)S(1)}, u32[]{:S(2)}, u32[]{:S(2)}) collective-permute-start(f32[4,1,128]{1,2,0:T(8,128)S(1)} %copy-done.2), channel_id=1, source_target_pairs={{0,1},{1,2},{2,3},{4,5},{5,6},{6,7},{8,9},{9,10},{10,11},{12,13},{... | collective-permute-start | bytes 6152 | tf_op jit(solution)/shard_map/ppermute | solution.py:359
  192.1 0.2 collective-permute-done.3
  192.3 1.3 collective-permute-start.5
  193.6 3.0 %collective-permute-start.4 = (f32[1,128,128]{1,2,0:T(8,128)S(1)}, f32[1,128,128]{1,2,0:T(8,128)S(1)}, u32[]{:S(2)}, u32[]{:S(2)}) collective-permute-start(f32[1,128,128]{1,2,0:T(8,128)S(1)} %copy-done.3), channel_id=1, source_target_pairs={{0,4},{4,8},{8,12},{12,16},{16,20},{20,24},{24,28},{28,32},{32,36}... | collective-permute-start | bytes 196616 | tf_op jit(solution)/shard_map/ppermute | solution.py:359
  196.7 0.2 fusion.4
  196.9 0.1 fusion.19
  197.1 0.1 fusion.20
  197.2 1.3 collective-permute-start.11
  198.5 0.0 collective-permute-done.7
  198.5 4.6 %collective-permute-start.10 = (f32[4,1,128]{1,2,0:T(8,128)S(1)}, f32[4,1,128]{1,2,0:T(8,128)S(1)}, u32[]{:S(2)}, u32[]{:S(2)}) collective-permute-start(f32[4,1,128]{1,2,0:T(8,128)S(1)} %get-tuple-element.24), channel_id=1, source_target_pairs={{0,1},{1,2},{2,3},{4,5},{5,6},{6,7},{8,9},{9,10},{10,11},{12,13},{... | collective-permute-start | bytes 6152 | tf_op jit(solution)/shard_map/ppermute | solution.py:359
  203.1 1.3 collective-permute-start.9
  204.4 0.0 collective-permute-done.5
  204.4 3.3 %collective-permute-start.8 = (f32[1,128,128]{1,2,0:T(8,128)S(1)}, f32[1,128,128]{1,2,0:T(8,128)S(1)}, u32[]{:S(2)}, u32[]{:S(2)}) collective-permute-start(f32[1,128,128]{1,2,0:T(8,128)S(1)} %get-tuple-element.20), channel_id=1, source_target_pairs={{0,4},{4,8},{8,12},{12,16},{16,20},{20,24},{24,28},{28,32},{32,36}... | collective-permute-start | bytes 196616 | tf_op jit(solution)/shard_map/ppermute | solution.py:359
  207.8 0.1 collective-permute-done.11
  207.9 1.8 collective-permute-done.10
  209.7 2.3 multiply_reduce_fusion
  212.0 5.7 %stack.39 = f32[9]{0:T(128)S(1)} concatenate(f32[1]{0:T(128)} %bitcast, f32[1]{0:T(128)} %bitcast.8, f32[1]{0:T(128)} %bitcast.9, f32[1]{0:T(128)} %bitcast.10, f32[1]{0:T(128)} %bitcast.11, f32[1]{0:T(128)} %bitcast.12, f32[1]{0:T(128)} %bitcast.13, f32[1]{0:T(128)} %bitcast.14, f32[1]{0:T(128)} %bitcast.15), dimensions={0} | concatenate | bytes 72 | tf_op jit(solution)/shard_map/stack | solution.py:388
  217.7 67.0 %psum.7 = f32[9]{0:T(128)S(1)} all-reduce(f32[9]{0:T(128)S(1)} %stack.39), channel_id=1, replica_groups=mesh['layer'=32,'split'=4] {'layer','split'}, use_global_device_ids=true, to_apply=%region_9.10 | all-reduce | flops 9 | bytes 72 | tf_op jit(solution)/shard_map/psum | solution.py:388
  284.8 0.7 fusion.32
  291.3 0.1 multiply_subtract_fusion
  291.4 0.8 copy.63
  292.2 0.8 copy.64
  (23 shorter events, 0.3 us)
Async XLA Ops:
  161.0 3.6 %copy-start = (f32[4,128,128]{2,1,0:T(8,128)S(1)}, f32[4,128,128]{2,1,0:T(8,128)}, u32[]{:S(2)}) copy-start(f32[4,128,128]{2,1,0:T(8,128)} %rhs_ref.1) | copy-start | bytes 786436
  161.0 11.5 %all-to-all-start = ((f32[4,1,16384]{2,1,0:T(1,128)}), f32[4,1,16384]{2,1,0:T(1,128)S(1)}, u32[]{:S(2)}, u32[]{:S(2)}) async-start(f32[4,1,16384]{2,1,0:T(1,128)} %reshape.6), calls=%async_computation | async-start | bytes 524288 | tf_op jit(solution)/shard_map/all_to_all | solution.py:378
  165.5 33.0 %collective-permute-start.7 = (f32[4,1,128]{1,2,0:T(8,128)}, f32[4,1,128]{1,2,0:T(8,128)}, u32[]{:S(2)}, u32[]{:S(2)}) collective-permute-start(f32[4,1,128]{1,2,0:T(8,128)} %copy.57), channel_id=1, source_target_pairs={{1,0},{2,1},{3,2},{5,4},{6,5},{7,6},{9,8},{10,9},{11,10},{13,12},{... | collective-permute-start | bytes 6152 | tf_op jit(solution)/shard_map/ppermute | solution.py:360
  167.1 1.0 copy-start.1
  175.6 18.0 %collective-permute-start = (f32[1,128,128]{1,2,0:T(8,128)S(1)}, f32[1,128,128]{1,2,0:T(8,128)S(1)}, u32[]{:S(2)}, u32[]{:S(2)}) collective-permute-start(f32[1,128,128]{1,2,0:T(8,128)S(1)} %get-tuple-element.49), channel_id=1, source_target_pairs={{0,4},{4,8},{8,12},{12,16},{16,20},{20,24},{24,28},{28,32},{32,36}... | collective-permute-start | bytes 196616 | tf_op jit(solution)/shard_map/ppermute | solution.py:359
  177.4 19.3 %collective-permute-start.1 = (f32[1,128,128]{1,2,0:T(8,128)S(1)}, f32[1,128,128]{1,2,0:T(8,128)S(1)}, u32[]{:S(2)}, u32[]{:S(2)}) collective-permute-start(f32[1,128,128]{1,2,0:T(8,128)S(1)} %get-tuple-element.48), channel_id=1, source_target_pairs={{4,0},{8,4},{12,8},{16,12},{20,16},{24,20},{28,24},{32,28},{36,32}... | collective-permute-start | bytes 196616 | tf_op jit(solution)/shard_map/ppermute | solution.py:360
  178.7 9.0 %collective-permute-start.2 = (f32[4,1,128]{1,2,0:T(8,128)S(1)}, f32[4,1,128]{1,2,0:T(8,128)S(1)}, u32[]{:S(2)}, u32[]{:S(2)}) collective-permute-start(f32[4,1,128]{1,2,0:T(8,128)S(1)} %get-tuple-element.45), channel_id=1, source_target_pairs={{0,1},{1,2},{2,3},{4,5},{5,6},{6,7},{8,9},{9,10},{10,11},{12,13},{... | collective-permute-start | bytes 6152 | tf_op jit(solution)/shard_map/ppermute | solution.py:359
  181.2 6.5 %copy-start.2 = (f32[4,1,128]{1,2,0:T(8,128)S(1)}, f32[4,1,128]{1,2,0:T(8,128)}, u32[]{:S(2)}) copy-start(f32[4,1,128]{1,2,0:T(8,128)} %copy.54) | copy-start | bytes 6148
  181.2 11.1 %copy-start.4 = (f32[1,128,128]{1,2,0:T(8,128)S(1)}, f32[1,128,128]{1,2,0:T(8,128)}, u32[]{:S(2)}) copy-start(f32[1,128,128]{1,2,0:T(8,128)} %get-tuple-element.31) | copy-start | bytes 196612
  181.2 12.4 %copy-start.3 = (f32[1,128,128]{1,2,0:T(8,128)S(1)}, f32[1,128,128]{1,2,0:T(8,128)}, u32[]{:S(2)}) copy-start(f32[1,128,128]{1,2,0:T(8,128)} %get-tuple-element.30) | copy-start | bytes 196612
  181.2 11.1 %collective-permute-start.3 = (f32[4,1,128]{1,2,0:T(8,128)S(1)}, f32[4,1,128]{1,2,0:T(8,128)S(1)}, u32[]{:S(2)}, u32[]{:S(2)}) collective-permute-start(f32[4,1,128]{1,2,0:T(8,128)S(1)} %get-tuple-element.44), channel_id=1, source_target_pairs={{1,0},{2,1},{3,2},{5,4},{6,5},{7,6},{9,8},{10,9},{11,10},{13,12},{... | collective-permute-start | bytes 6152 | tf_op jit(solution)/shard_map/ppermute | solution.py:360
  187.7 15.4 %collective-permute-start.6 = (f32[4,1,128]{1,2,0:T(8,128)S(1)}, f32[4,1,128]{1,2,0:T(8,128)S(1)}, u32[]{:S(2)}, u32[]{:S(2)}) collective-permute-start(f32[4,1,128]{1,2,0:T(8,128)S(1)} %copy-done.2), channel_id=1, source_target_pairs={{0,1},{1,2},{2,3},{4,5},{5,6},{6,7},{8,9},{9,10},{10,11},{12,13},{... | collective-permute-start | bytes 6152 | tf_op jit(solution)/shard_map/ppermute | solution.py:359
  192.3 12.1 %collective-permute-start.5 = (f32[1,128,128]{1,2,0:T(8,128)S(1)}, f32[1,128,128]{1,2,0:T(8,128)S(1)}, u32[]{:S(2)}, u32[]{:S(2)}) collective-permute-start(f32[1,128,128]{1,2,0:T(8,128)S(1)} %copy-done.4), channel_id=1, source_target_pairs={{4,0},{8,4},{12,8},{16,12},{20,16},{24,20},{28,24},{32,28},{36,32}... | collective-permute-start | bytes 196616 | tf_op jit(solution)/shard_map/ppermute | solution.py:360
  193.6 14.2 %collective-permute-start.4 = (f32[1,128,128]{1,2,0:T(8,128)S(1)}, f32[1,128,128]{1,2,0:T(8,128)S(1)}, u32[]{:S(2)}, u32[]{:S(2)}) collective-permute-start(f32[1,128,128]{1,2,0:T(8,128)S(1)} %copy-done.3), channel_id=1, source_target_pairs={{0,4},{4,8},{8,12},{12,16},{16,20},{20,24},{24,28},{28,32},{32,36}... | collective-permute-start | bytes 196616 | tf_op jit(solution)/shard_map/ppermute | solution.py:359
  197.2 10.7 %collective-permute-start.11 = (f32[4,1,128]{1,2,0:T(8,128)S(1)}, f32[4,1,128]{1,2,0:T(8,128)S(1)}, u32[]{:S(2)}, u32[]{:S(2)}) collective-permute-start(f32[4,1,128]{1,2,0:T(8,128)S(1)} %get-tuple-element.25), channel_id=1, source_target_pairs={{1,0},{2,1},{3,2},{5,4},{6,5},{7,6},{9,8},{10,9},{11,10},{13,12},{... | collective-permute-start | bytes 6152 | tf_op jit(solution)/shard_map/ppermute | solution.py:360
  198.5 11.1 %collective-permute-start.10 = (f32[4,1,128]{1,2,0:T(8,128)S(1)}, f32[4,1,128]{1,2,0:T(8,128)S(1)}, u32[]{:S(2)}, u32[]{:S(2)}) collective-permute-start(f32[4,1,128]{1,2,0:T(8,128)S(1)} %get-tuple-element.24), channel_id=1, source_target_pairs={{0,1},{1,2},{2,3},{4,5},{5,6},{6,7},{8,9},{9,10},{10,11},{12,13},{... | collective-permute-start | bytes 6152 | tf_op jit(solution)/shard_map/ppermute | solution.py:359
  203.1 6.5 %collective-permute-start.9 = (f32[1,128,128]{1,2,0:T(8,128)S(1)}, f32[1,128,128]{1,2,0:T(8,128)S(1)}, u32[]{:S(2)}, u32[]{:S(2)}) collective-permute-start(f32[1,128,128]{1,2,0:T(8,128)S(1)} %get-tuple-element.21), channel_id=1, source_target_pairs={{4,0},{8,4},{12,8},{16,12},{20,16},{24,20},{28,24},{32,28},{36,32}... | collective-permute-start | bytes 196616 | tf_op jit(solution)/shard_map/ppermute | solution.py:360
  204.4 5.2 %collective-permute-start.8 = (f32[1,128,128]{1,2,0:T(8,128)S(1)}, f32[1,128,128]{1,2,0:T(8,128)S(1)}, u32[]{:S(2)}, u32[]{:S(2)}) collective-permute-start(f32[1,128,128]{1,2,0:T(8,128)S(1)} %get-tuple-element.20), channel_id=1, source_target_pairs={{0,4},{4,8},{8,12},{12,16},{16,20},{20,24},{24,28},{28,32},{32,36}... | collective-permute-start | bytes 196616 | tf_op jit(solution)/shard_map/ppermute | solution.py:359

commit v2 on v1

--- a/solution.py
+++ b/solution.py
@@ -20,7 +20,11 @@
 def mm(x, w_high, w_low):
     high, low = split2(x)
     dot = functools.partial(jnp.dot, preferred_element_type=F32)
-    return dot(high, w_high) + (dot(low, w_high) + dot(high, w_low))
+    n = x.shape[0]
+    if n > 128:
+        return dot(high, w_high) + (dot(low, w_high) + dot(high, w_low))
+    both = dot(jnp.concatenate([high, low], 0), w_high)
+    return both[:n] + (both[n:] + dot(high, w_low))
 
 
 def mm_ref(x, pair):
@@ -34,11 +38,14 @@
 
 
 def sweep_kernel(
-    nlayer, nsplit, nchunk,
-    rhs_ref, inv_ref, out_ref,
-    gbuf, mats, rsend, cols, low, pf, qf, pown, qown, pall, qall, pin, qin,
+    nlayer, nsplit, nchunk, nrow,
+    rhs_ref, diag_ref, inv_ref, sol_ref, res_ref,
+    gbuf, mats, rsend, dsend, cols, dcols, low, dirb, imb, aimb, arb,
+    pf, qf, pown, qown, pall, qall, pin, qin,
     cvec, cin, ain, aout, amid, evec, ein, bin_, bout, bcore,
+    zlow, zhigh, ylow, yhigh, edges, lines, flat, part, group, whole,
     rs_send, rs_recv, g_send, g_recv, c_send, c_recv, d_send, d_recv, u_send, u_recv,
+    h_send, h_recv, l_send, l_recv, n_send, n_recv, w_send, w_recv,
 ):
     planes, nx, width = inv_ref.shape
     ysize = rhs_ref.shape[2]
@@ -59,6 +66,15 @@
     def rows(owner, start, size):
         return pl.ds(pl.multiple_of(owner * width + start, half), size)
 
+    def lanes(t):
+        return pl.ds(pl.multiple_of(t * width, width), width)
+
+    def lines_of(t):
+        return pl.ds(pl.multiple_of(t * yb, yb), yb)
+
+    for empty in (zlow, zhigh, ylow, yhigh, edges, part):
+        empty[...] = jnp.zeros_like(empty)
+
     barrier = pltpu.get_barrier_semaphore()
 
     def greet(l, t):
@@ -66,27 +82,26 @@
 
     for d in range(1, nsplit):
         greet(layer, lax.rem(s + d, nsplit))
-    greet(other, s)
-
-    @pl.when(jnp.logical_and(core == 0, jnp.logical_not(first)))
+    for d in range(nsplit):
+        greet(other, lax.rem(s + d, nsplit))
+    for d in range(1, nchip):
+        greet(2 * lax.rem(chip + d, nchip) + core, s)
+    side = layer - 1 + 2 * core
+    inner = jnp.logical_and(side >= 0, side < nlayer)
+
+    @pl.when(inner)
     def _():
-        greet(layer - 2, s)
-
-    @pl.when(jnp.logical_and(core == 0, jnp.logical_not(last)))
-    def _():
-        greet(layer + 2, s)
+        greet(side, s)
 
     for k in range(planes):
         gbuf[k, rows(s, 0, width), :] = inv_ref[k].T
-    for k in range(planes):
-        rsend[k] = rhs_ref[k].T
-    for k in range(planes):
-        cols[k, :, pl.ds(pl.multiple_of(s * width, width), width)] = rsend[
-            k, pl.ds(pl.multiple_of(s * yb, yb), yb), :
-        ]
-
-    ends = jnp.where(first, 1, 0) + jnp.where(last, 1, 0)
-    pl.semaphore_wait(barrier, nsplit + jnp.where(core == 0, 2 - ends, 0))
+    for source, sent, mine in ((rhs_ref, rsend, cols), (diag_ref, dsend, dcols)):
+        for k in range(planes):
+            sent[k] = source[k].T
+        for k in range(planes):
+            mine[k, :, lanes(s)] = sent[k, lines_of(s), :]
+
+    pl.semaphore_wait(barrier, 2 * nsplit - 1 + nchip - 1 + jnp.where(inner, 1, 0))
 
     def remote(src, dst, send, recv, l, t):
         return pltpu.make_async_remote_copy(
@@ -94,13 +109,94 @@
             device_id=(l, t), device_id_type=MESH,
         )
 
-    def regroup(d):
+    def regroup(n, d):
         t = lax.rem(s + d, nsplit)
-        return remote(
-            rsend.at[:, pl.ds(pl.multiple_of(t * yb, yb), yb), :],
-            cols.at[:, :, pl.ds(pl.multiple_of(s * width, width), width)],
-            rs_send.at[d - 1], rs_recv.at[d - 1], layer, t,
-        )
+        sent, mine = ((rsend, cols), (dsend, dcols))[n]
+        return remote(
+            sent.at[:, lines_of(t), :], mine.at[:, :, lanes(s)],
+            rs_send.at[n, d - 1], rs_recv.at[n, d - 1], layer, t,
+        )
+
+    def spread(n, d):
+        t = lax.rem(s + d, nsplit)
+        return remote(
+            (dirb, imb, aimb, arb)[n].at[:, :, lanes(t)], lines.at[n, :, lines_of(s), :],
+            l_send.at[n, d - 1], l_recv.at[n, d - 1], layer, t,
+        )
+
+    def spread_start(n):
+        for d in range(1, nsplit):
+            spread(n, d).start()
+        for k in range(planes):
+            lines[n, k, lines_of(s), :] = (dirb, imb, aimb, arb)[n][k, :, lanes(s)]
+
+    def spread_finish(n):
+        for d in range(1, nsplit):
+            spread(n, d).wait_recv()
+        for k in range(planes):
+            flat[n, k] = lines[n, k].T
+
+    def halo(n, i):
+        values = (cols, dirb, imb)[n]
+        src = (values.at[planes - 1], values.at[0], edges.at[n, 0], edges.at[n, 1])[i]
+        dst = (zlow, zhigh, ylow, yhigh)[i].at[n]
+        l, t = ((layer + 1, s), (layer - 1, s), (layer, s + 1), (layer, s - 1))[i]
+        return remote(src, dst, h_send.at[n, i], h_recv.at[n, i], l, t)
+
+    to_high, to_low = layer < nlayer - 1, layer > 0
+    to_right, to_left = s < nsplit - 1, s > 0
+    gives = (to_high, to_low, to_right, to_left)
+    takes = (to_low, to_high, to_left, to_right)
+
+    def halo_start(n):
+        values = (cols, dirb, imb)[n]
+        for i in range(2):
+            pl.when(gives[i])(lambda i=i: halo(n, i).start())
+        for k in range(planes):
+            edges[n, 0, k : k + 1, :] = values[k, yb - 1 : yb, :]
+            edges[n, 1, k : k + 1, :] = values[k, 0:1, :]
+        for i in range(2, 4):
+            pl.when(gives[i])(lambda i=i: halo(n, i).start())
+
+    def halo_wait(n):
+        for i in range(4):
+            pl.when(takes[i])(lambda i=i: halo(n, i).wait_recv())
+
+    row = lax.broadcasted_iota(jnp.int32, (yb, nx), 0)
+    lane = lax.broadcasted_iota(jnp.int32, (yb, nx), 1)
+
+    def apply_operator(n, result):
+        values = (cols, dirb, imb)[n]
+        for k in range(planes):
+            v = values[k]
+            below = values[k - 1] if k > 0 else zlow[n]
+            above = values[k + 1] if k < planes - 1 else zhigh[n]
+            x_low = jnp.where(lane == 0, 0.0, pltpu.roll(v, 1, 1))
+            x_high = jnp.where(lane == nx - 1, 0.0, pltpu.roll(v, nx - 1, 1))
+            y_low = jnp.where(row == 0, ylow[n, k : k + 1, :], pltpu.roll(v, 1, 0))
+            y_high = jnp.where(row == yb - 1, yhigh[n, k : k + 1, :], pltpu.roll(v, yb - 1, 0))
+            beside = (below + above) + (x_low + x_high) + (y_low + y_high)
+            result[k] = (6.0 + dcols[k]) * v - beside
+
+    def put_sum(i, a, b):
+        total = a[0] * b[0]
+        for k in range(1, planes):
+            total = total + a[k] * b[k]
+        total = jnp.sum(total, axis=0, keepdims=True)
+        lane_sum = total[:, :width]
+        for t in range(1, nsplit):
+            lane_sum = lane_sum + total[:, t * width : (t + 1) * width]
+        part[i : i + 1, :] = lane_sum
+
+    def prepare():
+        for d in range(1, nsplit):
+            regroup(1, d).wait_recv()
+        halo_wait(0)
+        apply_operator(0, arb)
+        spread_start(3)
+        put_sum(0, cols, cols)
+        put_sum(1, arb, cols)
+        put_sum(2, arb, arb)
 
     def own_right(k):
         part = gbuf.at[k, rows(s, 0, width), :]
@@ -119,7 +215,7 @@
         return remote(part, part, g_send.at[3, k], g_recv.at[3, k], layer, left)
 
     for d in range(1, nsplit):
-        regroup(d).start()
+        regroup(0, d).start()
     for k in range(min(2, planes)):
         own_right(k).start()
         own_left(k).start()
@@ -132,6 +228,9 @@
         if k + 2 < planes:
             own_right(k + 2).start()
             own_left(k + 2).start()
+        if k == planes - 1:
+            for d in range(1, nsplit):
+                regroup(1, d).start()
 
     def absorb(k):
         pass_right(k).wait_recv()
@@ -142,7 +241,8 @@
         mats[k, 1] = lowpart
         if k == 0:
             for d in range(1, nsplit):
-                regroup(d).wait_recv()
+                regroup(0, d).wait_recv()
+            halo_start(0)
             cvec[...] = mm(cols[0], high, lowpart)
             pf[...] = full
             qown[0] = high
@@ -213,11 +313,12 @@
                 state = low[k]
             else:
                 state = low[k] + mm(state, mats[k, 0], mats[k, 1])
-            out_ref[k] = state
+            dirb[k] = state
 
     @pl.when(core == 1)
     def _():
         give_q.start()
+        prepare()
         give_a.wait_recv()
         down_sweep(ain[pl.ds(0, yb), :])
         up_partial()
@@ -243,8 +344,12 @@
         store_pair(pown, pf[...])
         give_c.wait_recv()
         give_p.wait_recv()
-        store_pair(pin_pair := pall, pin[...])
-        aout[...] = mm_ref(cvec[...], pin_pair) + cin[...]
+        store_pair(pall, pin[...])
+        aout[...] = mm_ref(cvec[...], pall) + cin[...]
+
+        @pl.when(last)
+        def _():
+            prepare()
 
         @pl.when(first)
         def _():
@@ -256,7 +361,7 @@
 
         @pl.when(jnp.logical_not(first))
         def _():
-            product = mm_ref(pf[...], pin_pair)
+            product = mm_ref(pf[...], pall)
             store_pair(pall, product)
             for q in range(nchunk):
                 hand_down(q).wait_recv()
@@ -272,7 +377,7 @@
 
         up_partial()
         give_q.wait_recv()
-        store_pair(qin_pair := pown, qin[...])
+        store_pair(pown, qin[...])
         give_e.wait_recv()
         bout[...] = evec[...] + mm_ref(ein[...], qown)
 
@@ -285,6 +390,7 @@
         @pl.when(jnp.logical_not(last))
         def _():
             store_pair(qall, mm_ref(qin[...], qown))
+            prepare()
             for q in range(nchunk):
                 hand_up(q).wait_recv()
                 give_b(q).start()
@@ -294,7 +400,7 @@
                     bout[chunk(q), :] = bout[chunk(q), :] + mm_ref(bin_[chunk(q), :], qall)
                     hand_up(q).start()
 
-            up_sweep(ein[...] + mm_ref(bin_[...], qin_pair))
+            up_sweep(ein[...] + mm_ref(bin_[...], pown))
             for q in range(nchunk):
                 give_b(q).wait_send()
                 hand_down(q).wait_send()
@@ -306,94 +412,140 @@
 
         give_a.wait_send()
 
-    for d in range(1, nsplit):
-        regroup(d).wait_send()
+    halo_start(1)
+    spread_start(0)
+    halo_wait(1)
+    apply_operator(1, imb)
+    halo_start(2)
+    spread_start(1)
+    halo_wait(2)
+    apply_operator(2, aimb)
+    spread_start(2)
+    put_sum(3, cols, imb)
+    put_sum(4, arb, imb)
+    put_sum(5, aimb, cols)
+    put_sum(6, aimb, imb)
+    put_sum(7, arb, aimb)
+    put_sum(8, aimb, aimb)
+
+    place = core * nsplit + s
+    count = 2 * nsplit
+
+    def near(d):
+        at = lax.rem(place + d, count)
+        return remote(
+            group.at[place], group.at[place], n_send.at[d - 1], n_recv.at[d - 1],
+            2 * chip + at // nsplit, lax.rem(at, nsplit),
+        )
+
+    def far(d):
+        at = lax.rem(chip + d, nchip)
+        return remote(
+            whole.at[chip], whole.at[chip], w_send.at[d - 1], w_recv.at[d - 1],
+            2 * at + core, s,
+        )
+
+    group[place] = part[...]
+    for d in range(1, count):
+        near(d).start()
+    for n in (3, 0):
+        spread_finish(n)
+    for d in range(1, count):
+        near(d).wait_recv()
+    total = group[0]
+    for i in range(1, count):
+        total = total + group[i]
+    whole[chip] = total
+    for d in range(1, nchip):
+        far(d).start()
+    for n in (1, 2):
+        spread_finish(n)
+    for d in range(1, nchip):
+        far(d).wait_recv()
+    total = whole[0]
+    for i in range(1, nchip):
+        total = total + whole[i]
+    sums = jnp.sum(total, axis=1, keepdims=True)
+    rr, ar, aa, ri, ai, br, bi, ab, bb = [sums[i : i + 1, :] for i in range(9)]
+    alpha = rr / ri
+    cross = ar - alpha * (ai + br) + alpha * alpha * bi
+    own = aa - 2.0 * alpha * ab + alpha * alpha * bb
+    omega = cross / own
+    for k in range(planes):
+        middle = rhs_ref[k] - alpha * flat[1, k]
+        sol_ref[k] = alpha * flat[0, k] + omega * middle
+        res_ref[k] = middle - omega * (flat[3, k] - alpha * flat[2, k])
+
+    for n in range(2):
+        for d in range(1, nsplit):
+            regroup(n, d).wait_send()
     for k in range(planes):
         own_right(k).wait_send()
         own_left(k).wait_send()
         pass_right(k).wait_send()
         pass_left(k).wait_send()
-
-
-def sweeps(right_side, inverses, nlayer, nsplit):
+    for n in range(4):
+        for d in range(1, nsplit):
+            spread(n, d).wait_send()
+    for n in range(3):
+        for i in range(4):
+            pl.when(gives[i])(lambda n=n, i=i: halo(n, i).wait_send())
+    for d in range(1, count):
+        near(d).wait_send()
+    for d in range(1, nchip):
+        far(d).wait_send()
+
+
+def per_device(nlayer, nsplit, right_side, diagonal, inverses):
     planes, nx, width = inverses.shape
     ysize = right_side.shape[2]
     yb = ysize // nsplit
+    nchip = nlayer // 2
     nchunk = 2
+    nrow = 16
     vmem = pl.BlockSpec(memory_space=pltpu.VMEM)
     square = pltpu.VMEM((nx, nx), F32)
     pair = pltpu.VMEM((2, nx, nx), BF16)
     strip = pltpu.VMEM((yb, nx), F32)
+    columns = pltpu.VMEM((planes, yb, nx), F32)
+    block = pltpu.VMEM((planes, ysize, width), F32)
     dma = pltpu.SemaphoreType.DMA
+    shape = jax.ShapeDtypeStruct((planes, width, ysize), F32)
     return pl.pallas_call(
-        functools.partial(sweep_kernel, nlayer, nsplit, nchunk),
-        out_shape=jax.ShapeDtypeStruct((planes, yb, nx), F32),
-        in_specs=[vmem, vmem],
-        out_specs=vmem,
+        functools.partial(sweep_kernel, nlayer, nsplit, nchunk, nrow),
+        out_shape=(shape, shape),
+        in_specs=[vmem] * 3,
+        out_specs=(vmem, vmem),
         scratch_shapes=[
             pltpu.VMEM((planes, nx, nx), F32),
             pltpu.VMEM((planes, 2, nx, nx), BF16),
-            pltpu.VMEM((planes, ysize, width), F32),
-            pltpu.VMEM((planes, yb, nx), F32),
-            pltpu.VMEM((planes, yb, nx), F32),
+            block, block,
+            columns, columns, columns, columns, columns, columns, columns,
             square, square, pair, pair, pair, pair, square, square,
             strip, strip, strip, strip, strip, strip, strip, strip, strip, strip,
-            dma((nsplit - 1,)), dma((nsplit - 1,)),
+            pltpu.VMEM((3, yb, nx), F32), pltpu.VMEM((3, yb, nx), F32),
+            pltpu.VMEM((3, 8, nx), F32), pltpu.VMEM((3, 8, nx), F32),
+            pltpu.VMEM((3, 2, 8, nx), F32),
+            pltpu.VMEM((4, planes, ysize, width), F32),
+            pltpu.VMEM((4, planes, width, ysize), F32),
+            pltpu.VMEM((nrow, width), F32),
+            pltpu.VMEM((2 * nsplit, nrow, width), F32),
+            pltpu.VMEM((nchip, nrow, width), F32),
+            dma((2, nsplit - 1)), dma((2, nsplit - 1)),
             dma((4, planes)), dma((4, planes)),
             dma((5 + nchunk,)), dma((5 + nchunk,)),
             dma((nchunk,)), dma((nchunk,)),
             dma((nchunk,)), dma((nchunk,)),
+            dma((3, 4)), dma((3, 4)),
+            dma((4, nsplit - 1)), dma((4, nsplit - 1)),
+            dma((2 * nsplit - 1,)), dma((2 * nsplit - 1,)),
+            dma((nchip - 1,)), dma((nchip - 1,)),
         ],
         compiler_params=pltpu.CompilerParams(
             collective_id=0, has_side_effects=True, vmem_limit_bytes=56 * 1024 * 1024
         ),
         name="sweeps",
-    )(right_side, inverses)
-
-
-def shifted(x, axis, dim):
-    size, length = lax.axis_size(axis), x.shape[dim]
-    up = [(i, i + 1) for i in range(size - 1)]
-    last = lax.slice_in_dim(x, length - 1, length, axis=dim)
-    first = lax.slice_in_dim(x, 0, 1, axis=dim)
-    low = lax.ppermute(last, axis, up)
-    high = lax.ppermute(first, axis, [(b, a) for a, b in up])
-    return low, high
-
-
-def stencil(values, diagonal):
-    low0, high0 = shifted(values, "layer", 0)
-    low1, high1 = shifted(values, "split", 1)
-    beside = jnp.concatenate([low0, values[:-1]], 0) + jnp.concatenate([values[1:], high0], 0)
-    beside = beside + jnp.concatenate([low1, values[:, :-1]], 1)
-    beside = beside + jnp.concatenate([values[:, 1:], high1], 1)
-    y_upper = jnp.pad(values[:, :, 1:], ((0, 0), (0, 0), (0, 1)))
-    y_lower = jnp.pad(values[:, :, :-1], ((0, 0), (0, 0), (1, 0)))
-    return (6.0 + diagonal) * values - beside - y_upper - y_lower
-
-
-def per_device(nlayer, nsplit, right_side, diagonal, inverses):
-    applied_rhs = stencil(right_side, diagonal)
-    swept = sweeps(right_side, inverses, nlayer, nsplit)
-    regrouped = lax.all_to_all(swept, "split", split_axis=2, concat_axis=1, tiled=True)
-    direction = jnp.swapaxes(regrouped, 1, 2)
-    image = stencil(direction, diagonal)
-    applied_image = stencil(image, diagonal)
-    pairs = (
-        (right_side, right_side), (right_side, image),
-        (applied_rhs, right_side), (applied_rhs, image),
-        (applied_image, right_side), (applied_image, image),
-        (applied_rhs, applied_rhs), (applied_rhs, applied_image), (applied_image, applied_image),
-    )
-    sums = lax.psum(jnp.stack([jnp.sum(a * b) for a, b in pairs]), ("layer", "split"))
-    rr, ri, ar, ai, br, bi, aa, ab, bb = [sums[i] for i in range(9)]
-    alpha = rr / ri
-    middle = right_side - alpha * image
-    tangent = applied_rhs - alpha * applied_image
-    cross = ar - alpha * (ai + br) + alpha * alpha * bi
-    own = aa - 2.0 * alpha * ab + alpha * alpha * bb
-    omega = cross / own
-    return alpha * direction + omega * middle, middle - omega * tangent
+    )(right_side, diagonal, inverses)
 
 
 def solution(mesh):

time: 294 us -> 181 us (0.62)
  blocking collectives: 67 us -> 0 us
  starting transfers between devices: 31.1 us -> 0 us
  Pallas kernels: 158 us -> 177 us
  local copies, waits for them, and re-layouts: 16 us -> 2.42 us
  waiting for transfers between devices: 9.8 us -> 0 us
  between operations: 6.79 us -> 0.65 us
  other arithmetic: 4.68 us -> 0 us
    psum x1 -> x0, blocking collectives: 67 us -> none  [per_device(): lax.psum(jnp.stack([jnp.sum(a * b) for a, b in pairs]), ('layer', 'split'))]
    ppermute x12 -> x0, starting transfers between devices: 27.5 us -> none  [the longest x6 19.6 us: shifted(): low = lax.ppermute(last, axis, up)]
    pallas_call x1, Pallas kernels: 158 us -> 177 us  [per_device(): pl.pallas_call(functools.partial(sweep_kernel, nlayer, nsplit, nchunk, nr...]
    ppermute x12 -> x0, waiting for transfers between devices: 7.06 us -> none  [the longest x6 6.77 us: shifted(): low = lax.ppermute(last, axis, up)]
    another operation x1 -> x0, local copies, waits for them, and re-layouts: 5.73 us -> none  [per_device(): jnp.stack([jnp.sum(a * b) for a, b in pairs])]
    slice x18 -> x0, local copies, waits for them, and re-layouts: 3.94 us -> none  [the longest x5 1.66 us: shifted(): last = lax.slice_in_dim(x, length - 1, length, axis=dim)]
    all_to_all x1 -> x0, starting transfers between devices: 3.63 us -> none  [per_device(): lax.all_to_all(swept, 'split', split_axis=2, concat_axis=1, tiled=True)]
    reduce_sum x2 -> x0, other arithmetic: 2.99 us -> none  [per_device(): jnp.sum(a * b)]
  transfers between devices with their start and end apart: 13 -> 0, of which waited for: 5 -> 0; matrix products, arithmetic and copies ran while one was open for 2% -> 0% of each run, Pallas kernels for 0% -> 0%
where the time goes in v2:
time: 181 us; the launch traced here: 180 us
  Pallas kernels  177 us (98%)
  local copies, waits for them, and re-layouts  2.42 us (1%)
    pallas_call x1, Pallas kernels, per_device(): pl.pallas_call(functools.partial(sweep_kernel, nlayer, nsplit, nchunk, nr...  177 us

profile of v2, /device:TPU:0, one launch (start us, length us, event | category | flops | bytes accessed | tf_op | source)
XLA Modules:
  0.0 180.5 jit_solution(17462232776837243103)
XLA Ops:
  0.6 177.4 %sweeps.1 = (f32[4,128,128]{2,1,0:T(8,128)}, f32[4,128,128]{2,1,0:T(8,128)}) custom-call(f32[4,128,128]{2,1,0:T(8,128)} %rhs_ref.1, f32[4,128,128]{2,1,0:T(8,128)} %diag_ref.1, f32[4,512,128]{2,1,0:T(8,128)} %inv_ref.1), custom_call_target="tpu_custom_call" | custom-call | tf_op jit(solution)/shard_map/sweeps/pallas_call | solution.py:514
  178.0 0.0 copy-start
  178.0 1.7 copy.7
  179.7 0.0 copy-done
  179.7 0.7 copy.8
Async XLA Ops:
  178.0 1.7 copy-start

commit v3 on v2

--- a/solution.py
+++ b/solution.py
@@ -31,6 +31,11 @@
     return mm(x, pair[0], pair[1])
 
 
+def mm_pairs(x, pair):
+    dot = functools.partial(jnp.dot, preferred_element_type=F32)
+    return dot(x[0], pair[0]) + (dot(x[1], pair[0]) + dot(x[0], pair[1]))
+
+
 def store_pair(pair, x):
     high, low = split2(x)
     pair[0] = high
@@ -41,10 +46,12 @@
     nlayer, nsplit, nchunk, nrow,
     rhs_ref, diag_ref, inv_ref, sol_ref, res_ref,
     gbuf, mats, rsend, dsend, cols, dcols, low, dirb, imb, aimb, arb,
-    pf, qf, pown, qown, pall, qall, pin, qin,
-    cvec, cin, ain, aout, amid, evec, ein, bin_, bout, bcore,
+    pf, qf, pown, qown, pall, qall, q1, pin, qin,
+    cvec, cin, ain, amid, evec, ein, bin_, bcore, zin, zout,
+    xf, mbuf, xpair, xrow, vown, vbuf, inbuf,
     zlow, zhigh, ylow, yhigh, edges, lines, flat, part, group, whole,
-    rs_send, rs_recv, g_send, g_recv, c_send, c_recv, d_send, d_recv, u_send, u_recv,
+    rs_send, rs_recv, g_send, g_recv, c_send, c_recv,
+    x_send, x_recv, v_send, v_recv, i_send, i_recv, z_send, z_recv, y_send, y_recv,
     h_send, h_recv, l_send, l_recv, n_send, n_recv, w_send, w_recv,
 ):
     planes, nx, width = inv_ref.shape
@@ -60,8 +67,9 @@
     right = lax.rem(s + 1, nsplit)
     left = lax.rem(s + nsplit - 1, nsplit)
     other = layer + 1 - 2 * core
-    first = chip == 0
-    last = chip == nchip - 1
+    npos = 4
+    pos, line = lax.rem(chip, npos), chip // npos
+    nline = nchip // npos
 
     def rows(owner, start, size):
         return pl.ds(pl.multiple_of(owner * width + start, half), size)
@@ -266,27 +274,124 @@
     give_p = remote(pf, pin, c_send.at[0], c_recv.at[0], other, s)
     give_q = remote(qf, qin, c_send.at[1], c_recv.at[1], other, s)
     give_c = remote(cvec, cin, c_send.at[2], c_recv.at[2], other, s)
-    give_a = remote(amid, ain.at[pl.ds(0, yb), :], c_send.at[3], c_recv.at[3], other, s)
+    give_a = remote(amid, ain, c_send.at[3], c_recv.at[3], other, s)
     give_e = remote(evec, ein, c_send.at[4], c_recv.at[4], other, s)
+    give_b = remote(bin_, bcore, c_send.at[5], c_recv.at[5], other, s)
+
+    hosts = (npos - 1, 0)
+
+    def row_layer(at):
+        return 2 * (line * npos + at)
 
     def chunk(q):
         return pl.ds(q * cb, cb)
 
-    def give_b(q):
-        return remote(
-            bin_.at[chunk(q), :], bcore.at[chunk(q), :],
-            c_send.at[5 + q], c_recv.at[5 + q], other, s,
-        )
-
-    def hand_down(q):
-        return remote(
-            aout.at[chunk(q), :], ain.at[chunk(q), :], d_send.at[q], d_recv.at[q], layer + 2, s
-        )
-
-    def hand_up(q):
-        return remote(
-            bout.at[chunk(q), :], bin_.at[chunk(q), :], u_send.at[q], u_recv.at[q], layer - 2, s
-        )
+    def hand_matrix(way, step):
+        part = xf.at[way], mbuf.at[step]
+        if step == 1:
+            part = tuple(ref.at[rows(s, 0, width), :] for ref in part)
+        return remote(*part, x_send.at[way], x_recv.at[step], row_layer(hosts[way]), s)
+
+    def hand_vector(way, step):
+        return remote(
+            vown.at[way], vbuf.at[step], v_send.at[way], v_recv.at[step],
+            row_layer(hosts[way]), s,
+        )
+
+    def hand_input(way, step):
+        return remote(
+            inbuf.at[step], (ain, bin_)[way], i_send.at[step], i_recv.at[way],
+            row_layer(step if way == 0 else npos - 1 - step), s,
+        )
+
+    def hand_on(way, q):
+        return remote(
+            zout.at[chunk(q), :], zin.at[chunk(q), :], z_send.at[q], z_recv.at[q],
+            layer + (2 - 4 * way) * npos, s,
+        )
+
+    def ring(i):
+        owner, start, size = ((s, 0, width), (s, 0, width), (left, 0, half), (right, half, half))[i]
+        part = mbuf.at[1, rows(owner, start, size), :]
+        return remote(
+            part, part, y_send.at[i], y_recv.at[i], layer, (right, left, right, left)[i]
+        )
+
+    def for_step(way, do):
+        for step in range(npos - 1):
+            at = step if way == 0 else npos - 1 - step
+            pl.when(pos == at)(functools.partial(do, step))
+
+    def host_prepare(way):
+        store_pair(pall if way == 0 else qall, xf[way])
+        own = pall if way == 0 else qall
+        hand_matrix(way, 1).wait_recv()
+        ring(0).start()
+        ring(1).start()
+        hand_matrix(way, 0).wait_recv()
+        store_pair(xpair.at[0], mbuf[0])
+        ring(0).wait_recv()
+        ring(2).start()
+        ring(1).wait_recv()
+        ring(3).start()
+        ring(2).wait_recv()
+        ring(3).wait_recv()
+        store_pair(xpair.at[1], mbuf[1])
+        store_pair(xrow, mm_ref(mbuf[0], xpair.at[1]))
+        hand_matrix(way, 2).wait_recv()
+        store_pair(xpair.at[2], mbuf[2])
+        mbuf[2] = mm_pairs(xrow, xpair.at[2])
+        store_pair(xrow, mm_ref(mbuf[2], own))
+
+    def host_chain(way):
+        own = pall if way == 0 else qall
+        starts = line == 0 if way == 0 else line == nline - 1
+        ends = line == nline - 1 if way == 0 else line == 0
+        for step in range(npos - 1):
+            hand_vector(way, step).wait_recv()
+        total = vbuf[0]
+        for step in range(1, npos - 1):
+            total = vbuf[step] + mm_ref(total, xpair.at[step])
+        zout[...] = vown[way] + mm_ref(total, own)
+
+        @pl.when(starts)
+        def _():
+            inbuf[0] = jnp.zeros((yb, nx), F32)
+            if nline > 1:
+                for q in range(nchunk):
+                    hand_on(way, q).start()
+
+        @pl.when(jnp.logical_not(starts))
+        def _():
+            for q in range(nchunk):
+                hand_on(way, q).wait_recv()
+
+                @pl.when(jnp.logical_not(ends))
+                def _():
+                    zout[chunk(q), :] = zout[chunk(q), :] + mm_ref(zin[chunk(q), :], xrow)
+                    hand_on(way, q).start()
+
+            inbuf[0] = zin[...]
+
+        state = inbuf[0]
+        for step in range(npos - 1):
+            hand_input(way, step).start()
+            state = vbuf[step] + mm_ref(state, xpair.at[step])
+            if step < npos - 2:
+                inbuf[step + 1] = state
+        (ain, bin_)[way][...] = state
+
+    def host_finish(way):
+        ends = line == nline - 1 if way == 0 else line == 0
+        for step in range(npos - 1):
+            hand_input(way, step).wait_send()
+        for i in range(4):
+            ring(i).wait_send()
+
+        @pl.when(jnp.logical_not(ends))
+        def _():
+            for q in range(nchunk):
+                hand_on(way, q).wait_send()
 
     @pl.when(core == 1)
     def _():
@@ -297,8 +402,7 @@
 
     def down_sweep(state):
         for k in range(planes):
-            source = cols[k] if state is None else cols[k] + state
-            state = mm(source, mats[k, 0], mats[k, 1])
+            state = mm(cols[k] + state, mats[k, 0], mats[k, 1])
             low[k] = state
 
     def up_partial():
@@ -309,10 +413,7 @@
 
     def up_sweep(state):
         for k in range(planes - 1, -1, -1):
-            if state is None:
-                state = low[k]
-            else:
-                state = low[k] + mm(state, mats[k, 0], mats[k, 1])
+            state = low[k] + mm(state, mats[k, 0], mats[k, 1])
             dirb[k] = state
 
     @pl.when(core == 1)
@@ -320,20 +421,11 @@
         give_q.start()
         prepare()
         give_a.wait_recv()
-        down_sweep(ain[pl.ds(0, yb), :])
+        down_sweep(ain[...])
         up_partial()
         give_e.start()
-
-        @pl.when(last)
-        def _():
-            up_sweep(None)
-
-        @pl.when(jnp.logical_not(last))
-        def _():
-            for q in range(nchunk):
-                give_b(q).wait_recv()
-            up_sweep(bcore[...])
-
+        give_b.wait_recv()
+        up_sweep(bcore[...])
         give_c.wait_send()
         give_p.wait_send()
         give_q.wait_send()
@@ -345,72 +437,47 @@
         give_c.wait_recv()
         give_p.wait_recv()
         store_pair(pall, pin[...])
-        aout[...] = mm_ref(cvec[...], pall) + cin[...]
-
-        @pl.when(last)
+        vown[0] = mm_ref(cvec[...], pall) + cin[...]
+        for_step(0, lambda step: hand_vector(0, step).start())
+        xf[0] = mm_pairs(pown, pall)
+        for_step(0, lambda step: hand_matrix(0, step).start())
+        give_q.wait_recv()
+        store_pair(q1, qin[...])
+        xf[1] = mm_pairs(q1, qown)
+        for_step(1, lambda step: hand_matrix(1, step).start())
+        prepare()
+
+        @pl.when(pos == hosts[0])
         def _():
-            prepare()
-
-        @pl.when(first)
+            host_prepare(0)
+            host_chain(0)
+
+        @pl.when(pos == hosts[1])
         def _():
-            for q in range(nchunk):
-                hand_down(q).start()
-            amid[...] = cvec[...]
-            give_a.start()
-            down_sweep(None)
-
-        @pl.when(jnp.logical_not(first))
+            host_prepare(1)
+
+        for_step(0, lambda step: hand_input(0, step).wait_recv())
+        amid[...] = cvec[...] + mm_ref(ain[...], pown)
+        give_a.start()
+        down_sweep(ain[...])
+        up_partial()
+        give_e.wait_recv()
+        vown[1] = evec[...] + mm_ref(ein[...], qown)
+        for_step(1, lambda step: hand_vector(1, step).start())
+
+        @pl.when(pos == hosts[1])
         def _():
-            product = mm_ref(pf[...], pall)
-            store_pair(pall, product)
-            for q in range(nchunk):
-                hand_down(q).wait_recv()
-                aout[chunk(q), :] = aout[chunk(q), :] + mm_ref(ain[chunk(q), :], pall)
-
-                @pl.when(jnp.logical_not(last))
-                def _():
-                    hand_down(q).start()
-
-            amid[...] = cvec[...] + mm_ref(ain[pl.ds(0, yb), :], pown)
-            give_a.start()
-            down_sweep(ain[pl.ds(0, yb), :])
-
-        up_partial()
-        give_q.wait_recv()
-        store_pair(pown, qin[...])
-        give_e.wait_recv()
-        bout[...] = evec[...] + mm_ref(ein[...], qown)
-
-        @pl.when(last)
-        def _():
-            for q in range(nchunk):
-                hand_up(q).start()
-            up_sweep(ein[...])
-
-        @pl.when(jnp.logical_not(last))
-        def _():
-            store_pair(qall, mm_ref(qin[...], qown))
-            prepare()
-            for q in range(nchunk):
-                hand_up(q).wait_recv()
-                give_b(q).start()
-
-                @pl.when(jnp.logical_not(first))
-                def _():
-                    bout[chunk(q), :] = bout[chunk(q), :] + mm_ref(bin_[chunk(q), :], qall)
-                    hand_up(q).start()
-
-            up_sweep(ein[...] + mm_ref(bin_[...], pown))
-            for q in range(nchunk):
-                give_b(q).wait_send()
-                hand_down(q).wait_send()
-
-        @pl.when(jnp.logical_not(first))
-        def _():
-            for q in range(nchunk):
-                hand_up(q).wait_send()
-
+            host_chain(1)
+
+        for_step(1, lambda step: hand_input(1, step).wait_recv())
+        give_b.start()
+        up_sweep(ein[...] + mm_ref(bin_[...], q1))
         give_a.wait_send()
+        give_b.wait_send()
+        for way in range(2):
+            for_step(way, lambda step, way=way: hand_vector(way, step).wait_send())
+            for_step(way, lambda step, way=way: hand_matrix(way, step).wait_send())
+            pl.when(pos == hosts[way])(functools.partial(host_finish, way))
 
     halo_start(1)
     spread_start(0)
@@ -521,8 +588,12 @@
             pltpu.VMEM((planes, 2, nx, nx), BF16),
             block, block,
             columns, columns, columns, columns, columns, columns, columns,
-            square, square, pair, pair, pair, pair, square, square,
+            square, square, pair, pair, pair, pair, pair, square, square,
             strip, strip, strip, strip, strip, strip, strip, strip, strip, strip,
+            pltpu.VMEM((2, nx, nx), F32), pltpu.VMEM((3, nx, nx), F32),
+            pltpu.VMEM((3, 2, nx, nx), BF16), pair,
+            pltpu.VMEM((2, yb, nx), F32), pltpu.VMEM((3, yb, nx), F32),
+            pltpu.VMEM((3, yb, nx), F32),
             pltpu.VMEM((3, yb, nx), F32), pltpu.VMEM((3, yb, nx), F32),
             pltpu.VMEM((3, 8, nx), F32), pltpu.VMEM((3, 8, nx), F32),
             pltpu.VMEM((3, 2, 8, nx), F32),
@@ -533,9 +604,9 @@
             pltpu.VMEM((nchip, nrow, width), F32),
             dma((2, nsplit - 1)), dma((2, nsplit - 1)),
             dma((4, planes)), dma((4, planes)),
-            dma((5 + nchunk,)), dma((5 + nchunk,)),
-            dma((nchunk,)), dma((nchunk,)),
-            dma((nchunk,)), dma((nchunk,)),
+            dma((6,)), dma((6,)),
+            dma((2,)), dma((3,)), dma((2,)), dma((3,)), dma((3,)), dma((2,)),
+            dma((nchunk,)), dma((nchunk,)), dma((4,)), dma((4,)),
             dma((3, 4)), dma((3, 4)),
             dma((4, nsplit - 1)), dma((4, nsplit - 1)),
             dma((2 * nsplit - 1,)), dma((2 * nsplit - 1,)),

time: 181 us -> 141 us (0.78)
  Pallas kernels: 177 us -> 137 us
    pallas_call x1, Pallas kernels: 177 us -> 137 us  [per_device(): pl.pallas_call(functools.partial(sweep_kernel, nlayer, nsplit, nchunk, nr...]
where the time goes in v3:
time: 141 us
  Pallas kernels  137 us (97%)
  local copies, waits for them, and re-layouts  2.42 us (2%)
    pallas_call x1, Pallas kernels, per_device(): pl.pallas_call(functools.partial(sweep_kernel, nlayer, nsplit, nchunk, nr...  137 us

profile of v3, /device:TPU:0, one launch (start us, length us, event | category | flops | bytes accessed | tf_op | source)
XLA Modules:
  0.0 140.5 jit_solution(17933403870360962005)
XLA Ops:
  0.6 137.5 %sweeps.1 = (f32[4,128,128]{2,1,0:T(8,128)}, f32[4,128,128]{2,1,0:T(8,128)}) custom-call(f32[4,128,128]{2,1,0:T(8,128)} %rhs_ref.1, f32[4,128,128]{2,1,0:T(8,128)} %diag_ref.1, f32[4,512,128]{2,1,0:T(8,128)} %inv_ref.1), custom_call_target="tpu_custom_call" | custom-call | tf_op jit(solution)/shard_map/sweeps/pallas_call | solution.py:581
  138.1 0.0 copy-start
  138.1 1.7 %copy.7 = f32[4,128,128]{2,1,0:T(8,128)} copy(f32[4,128,128]{2,1,0:T(8,128)} %get-tuple-element.4) | data formatting | bytes 524288
  139.8 0.0 copy-done
  139.8 0.7 copy.8
Async XLA Ops:
  138.1 1.7 %copy-start = (f32[4,128,128]{2,1,0:T(8,128)S(1)}, f32[4,128,128]{2,1,0:T(8,128)}, u32[]{:S(2)}) copy-start(f32[4,128,128]{2,1,0:T(8,128)} %get-tuple-element.5) | copy-start | bytes 786436

commit v4 on v3

--- a/solution.py
+++ b/solution.py
@@ -49,6 +49,7 @@
     pf, qf, pown, qown, pall, qall, q1, pin, qin,
     cvec, cin, ain, amid, evec, ein, bin_, bcore, zin, zout,
     xf, mbuf, xpair, xrow, vown, vbuf, inbuf,
+    prefix, rf, rin, rpair, azero, ezero, ein0,
     zlow, zhigh, ylow, yhigh, edges, lines, flat, part, group, whole,
     rs_send, rs_recv, g_send, g_recv, c_send, c_recv,
     x_send, x_recv, v_send, v_recv, i_send, i_recv, z_send, z_recv, y_send, y_recv,
@@ -257,6 +258,7 @@
             qown[1] = lowpart
         else:
             cvec[...] = mm(cols[k] + cvec[...], high, lowpart)
+            prefix[k - 1] = pf[...]
             pf[...] = mm(pf[...], high, lowpart)
 
     def absorb_up(k):
@@ -277,6 +279,9 @@
     give_a = remote(amid, ain, c_send.at[3], c_recv.at[3], other, s)
     give_e = remote(evec, ein, c_send.at[4], c_recv.at[4], other, s)
     give_b = remote(bin_, bcore, c_send.at[5], c_recv.at[5], other, s)
+    give_r = remote(rf, rin, c_send.at[6], c_recv.at[6], other, s)
+    give_a0 = remote(cvec, azero, c_send.at[7], c_recv.at[7], other, s)
+    give_e0 = remote(ezero, ein0, c_send.at[8], c_recv.at[8], other, s)
 
     hosts = (npos - 1, 0)
 
@@ -286,11 +291,28 @@
     def chunk(q):
         return pl.ds(q * cb, cb)
 
-    def hand_matrix(way, step):
-        part = xf.at[way], mbuf.at[step]
-        if step == 1:
-            part = tuple(ref.at[rows(s, 0, width), :] for ref in part)
-        return remote(*part, x_send.at[way], x_recv.at[step], row_layer(hosts[way]), s)
+    def shared(step):
+        return (0, width) if step == 1 else (nx // 2, width // 2)
+
+    def hand_share(way, step):
+        base, size = shared(step)
+        part = pl.ds(pl.multiple_of(base + s * size, size), size)
+        return remote(
+            xf.at[way, part, :], mbuf.at[step, part, :],
+            x_send.at[way, 0], x_recv.at[step, 0], row_layer(hosts[way]), s,
+        )
+
+    def hand_whole(way, step):
+        part = pl.ds(0, nx // 2)
+        return remote(
+            xf.at[way, part, :], mbuf.at[step, part, :],
+            x_send.at[way, 1], x_recv.at[step, 1], row_layer(hosts[way]), s,
+        )
+
+    def hand_wholes(way, do):
+        for step in (0, 2):
+            at = step if way == 0 else npos - 1 - step
+            pl.when(pos == at)(functools.partial(do, step))
 
     def hand_vector(way, step):
         return remote(
@@ -310,11 +332,16 @@
             layer + (2 - 4 * way) * npos, s,
         )
 
-    def ring(i):
-        owner, start, size = ((s, 0, width), (s, 0, width), (left, 0, half), (right, half, half))[i]
-        part = mbuf.at[1, rows(owner, start, size), :]
-        return remote(
-            part, part, y_send.at[i], y_recv.at[i], layer, (right, left, right, left)[i]
+    def ring(step, i):
+        base, size = shared(step)
+        owner, start, length = (
+            (s, 0, size), (s, 0, size), (left, 0, size // 2), (right, size // 2, size // 2)
+        )[i]
+        rows_at = pl.multiple_of(base + owner * size + start, size // 2)
+        part = mbuf.at[step, pl.ds(rows_at, length), :]
+        return remote(
+            part, part, y_send.at[step, i], y_recv.at[step, i], layer,
+            (right, left, right, left)[i],
         )
 
     def for_step(way, do):
@@ -323,25 +350,37 @@
             pl.when(pos == at)(functools.partial(do, step))
 
     def host_prepare(way):
-        store_pair(pall if way == 0 else qall, xf[way])
         own = pall if way == 0 else qall
-        hand_matrix(way, 1).wait_recv()
-        ring(0).start()
-        ring(1).start()
-        hand_matrix(way, 0).wait_recv()
-        store_pair(xpair.at[0], mbuf[0])
-        ring(0).wait_recv()
-        ring(2).start()
-        ring(1).wait_recv()
-        ring(3).start()
-        ring(2).wait_recv()
-        ring(3).wait_recv()
-        store_pair(xpair.at[1], mbuf[1])
-        store_pair(xrow, mm_ref(mbuf[0], xpair.at[1]))
-        hand_matrix(way, 2).wait_recv()
-        store_pair(xpair.at[2], mbuf[2])
-        mbuf[2] = mm_pairs(xrow, xpair.at[2])
-        store_pair(xrow, mm_ref(mbuf[2], own))
+        store_pair(own, xf[way])
+        order = (1, 0, 2)
+        for step in order:
+            hand_share(way, step).wait_recv()
+            ring(step, 0).start()
+            ring(step, 1).start()
+        for step in order:
+            ring(step, 0).wait_recv()
+            ring(step, 2).start()
+            ring(step, 1).wait_recv()
+            ring(step, 3).start()
+        upper, lower = pl.ds(0, nx // 2), pl.ds(nx // 2, nx // 2)
+        for step in order:
+            ring(step, 2).wait_recv()
+            ring(step, 3).wait_recv()
+            if step == 1:
+                store_pair(xpair.at[1], mbuf[1])
+            if step == 0:
+                pf[lower, :] = mm_ref(mbuf[0, lower, :], xpair.at[1])
+            if step == 2:
+                pin[lower, :] = mm_ref(mbuf[2, lower, :], own)
+        hand_whole(way, 0).wait_recv()
+        pf[upper, :] = mm_ref(mbuf[0, upper, :], xpair.at[1])
+        hand_whole(way, 2).wait_recv()
+        pin[upper, :] = mm_ref(mbuf[2, upper, :], own)
+        store_pair(xrow, pin[...])
+        pf[...] = mm_ref(pf[...], xrow)
+        store_pair(xrow, pf[...])
+        for step in (0, 2):
+            store_pair(xpair.at[step], mbuf[step])
 
     def host_chain(way):
         own = pall if way == 0 else qall
@@ -385,8 +424,9 @@
         ends = line == nline - 1 if way == 0 else line == 0
         for step in range(npos - 1):
             hand_input(way, step).wait_send()
-        for i in range(4):
-            ring(i).wait_send()
+        for step in range(npos - 1):
+            for i in range(4):
+                ring(step, i).wait_send()
 
         @pl.when(jnp.logical_not(ends))
         def _():
@@ -405,11 +445,16 @@
             state = mm(cols[k] + state, mats[k, 0], mats[k, 1])
             low[k] = state
 
-    def up_partial():
+    def up_partial(result):
         state = low[planes - 1]
         for k in range(planes - 2, -1, -1):
             state = low[k] + mm(state, mats[k, 0], mats[k, 1])
-        evec[...] = state
+        result[...] = state
+
+    def response():
+        rf[...] = prefix[planes - 2] + mm(pf[...], mats[planes - 2, 0], mats[planes - 2, 1])
+        for k in range(planes - 3, -1, -1):
+            rf[...] = prefix[k] + mm(rf[...], mats[k, 0], mats[k, 1])
 
     def up_sweep(state):
         for k in range(planes - 1, -1, -1):
@@ -419,20 +464,25 @@
     @pl.when(core == 1)
     def _():
         give_q.start()
+        response()
+        give_r.start()
+        give_a0.wait_recv()
+        down_sweep(azero[...])
+        up_partial(ezero)
+        give_e0.start()
         prepare()
         give_a.wait_recv()
         down_sweep(ain[...])
-        up_partial()
+        up_partial(evec)
         give_e.start()
         give_b.wait_recv()
         up_sweep(bcore[...])
-        give_c.wait_send()
-        give_p.wait_send()
-        give_q.wait_send()
-        give_e.wait_send()
+        for give in (give_c, give_p, give_q, give_r, give_e0, give_e):
+            give.wait_send()
 
     @pl.when(core == 0)
     def _():
+        give_a0.start()
         store_pair(pown, pf[...])
         give_c.wait_recv()
         give_p.wait_recv()
@@ -440,43 +490,75 @@
         vown[0] = mm_ref(cvec[...], pall) + cin[...]
         for_step(0, lambda step: hand_vector(0, step).start())
         xf[0] = mm_pairs(pown, pall)
-        for_step(0, lambda step: hand_matrix(0, step).start())
+        for_step(0, lambda step: hand_share(0, step).start())
         give_q.wait_recv()
         store_pair(q1, qin[...])
         xf[1] = mm_pairs(q1, qown)
-        for_step(1, lambda step: hand_matrix(1, step).start())
+        for_step(1, lambda step: hand_share(1, step).start())
+        hand_wholes(0, lambda step: hand_whole(0, step).start())
+        hand_wholes(1, lambda step: hand_whole(1, step).start())
         prepare()
 
         @pl.when(pos == hosts[0])
         def _():
+            give_r.wait_recv()
+            give_e0.wait_recv()
             host_prepare(0)
             host_chain(0)
 
+        @pl.when(pos != hosts[0])
+        def _():
+            response()
+            give_r.wait_recv()
+            store_pair(rpair, rin[...])
+            rin[...] = mm_ref(pf[...], rpair)
+            rf[...] = rf[...] + mm_ref(rin[...], qown)
+            store_pair(rpair, rf[...])
+            down_sweep(jnp.zeros((yb, nx), F32))
+            up_partial(ezero)
+            give_e0.wait_recv()
+            ezero[...] = ezero[...] + mm_ref(ein0[...], qown)
+
         @pl.when(pos == hosts[1])
         def _():
             host_prepare(1)
 
         for_step(0, lambda step: hand_input(0, step).wait_recv())
+
+        @pl.when(pos != hosts[0])
+        def _():
+            vown[1] = ezero[...] + mm_ref(ain[...], rpair)
+            for_step(1, lambda step: hand_vector(1, step).start())
+
         amid[...] = cvec[...] + mm_ref(ain[...], pown)
         give_a.start()
         down_sweep(ain[...])
-        up_partial()
-        give_e.wait_recv()
-        vown[1] = evec[...] + mm_ref(ein[...], qown)
-        for_step(1, lambda step: hand_vector(1, step).start())
+
+        @pl.when(pos == hosts[0])
+        def _():
+            up_partial(evec)
+            give_e.wait_recv()
+            vown[1] = evec[...] + mm_ref(ein[...], qown)
+            hand_vector(1, 0).start()
 
         @pl.when(pos == hosts[1])
         def _():
             host_chain(1)
+
+        @pl.when(pos != hosts[0])
+        def _():
+            give_e.wait_recv()
 
         for_step(1, lambda step: hand_input(1, step).wait_recv())
         give_b.start()
         up_sweep(ein[...] + mm_ref(bin_[...], q1))
+        give_a0.wait_send()
         give_a.wait_send()
         give_b.wait_send()
         for way in range(2):
             for_step(way, lambda step, way=way: hand_vector(way, step).wait_send())
-            for_step(way, lambda step, way=way: hand_matrix(way, step).wait_send())
+            for_step(way, lambda step, way=way: hand_share(way, step).wait_send())
+            hand_wholes(way, lambda step, way=way: hand_whole(way, step).wait_send())
             pl.when(pos == hosts[way])(functools.partial(host_finish, way))
 
     halo_start(1)
@@ -594,6 +676,7 @@
             pltpu.VMEM((3, 2, nx, nx), BF16), pair,
             pltpu.VMEM((2, yb, nx), F32), pltpu.VMEM((3, yb, nx), F32),
             pltpu.VMEM((3, yb, nx), F32),
+            pltpu.VMEM((planes - 1, nx, nx), F32), square, square, pair, strip, strip, strip,
             pltpu.VMEM((3, yb, nx), F32), pltpu.VMEM((3, yb, nx), F32),
             pltpu.VMEM((3, 8, nx), F32), pltpu.VMEM((3, 8, nx), F32),
             pltpu.VMEM((3, 2, 8, nx), F32),
@@ -604,9 +687,9 @@
             pltpu.VMEM((nchip, nrow, width), F32),
             dma((2, nsplit - 1)), dma((2, nsplit - 1)),
             dma((4, planes)), dma((4, planes)),
-            dma((6,)), dma((6,)),
-            dma((2,)), dma((3,)), dma((2,)), dma((3,)), dma((3,)), dma((2,)),
-            dma((nchunk,)), dma((nchunk,)), dma((4,)), dma((4,)),
+            dma((9,)), dma((9,)),
+            dma((2, 2)), dma((3, 2)), dma((2,)), dma((3,)), dma((3,)), dma((2,)),
+            dma((nchunk,)), dma((nchunk,)), dma((3, 4)), dma((3, 4)),
             dma((3, 4)), dma((3, 4)),
             dma((4, nsplit - 1)), dma((4, nsplit - 1)),
             dma((2 * nsplit - 1,)), dma((2 * nsplit - 1,)),

time: 141 us -> 135 us (0.957)
  Pallas kernels: 137 us -> 131 us
    pallas_call x1, Pallas kernels: 137 us -> 131 us  [per_device(): pl.pallas_call(functools.partial(sweep_kernel, nlayer, nsplit, nchunk, nr...]
where the time goes in v4:
time: 135 us; the launch traced here: 134 us
  Pallas kernels  131 us (97%)
  local copies, waits for them, and re-layouts  2.42 us (2%)
    pallas_call x1, Pallas kernels, per_device(): pl.pallas_call(functools.partial(sweep_kernel, nlayer, nsplit, nchunk, nr...  131 us

profile of v4, /device:TPU:0, one launch (start us, length us, event | category | flops | bytes accessed | tf_op | source)
XLA Modules:
  0.0 134.1 jit_solution(3913386841702921054)
XLA Ops:
  0.6 131.0 %sweeps.1 = (f32[4,128,128]{2,1,0:T(8,128)}, f32[4,128,128]{2,1,0:T(8,128)}) custom-call(f32[4,128,128]{2,1,0:T(8,128)} %rhs_ref.1, f32[4,128,128]{2,1,0:T(8,128)} %diag_ref.1, f32[4,512,128]{2,1,0:T(8,128)} %inv_ref.1), custom_call_target="tpu_custom_call" | custom-call | tf_op jit(solution)/shard_map/sweeps/pallas_call | solution.py:663
  131.6 0.0 copy-start
  131.6 1.7 %copy.7 = f32[4,128,128]{2,1,0:T(8,128)} copy(f32[4,128,128]{2,1,0:T(8,128)} %get-tuple-element.4) | data formatting | bytes 524288
  133.4 0.0 copy-done
  133.4 0.7 copy.8
Async XLA Ops:
  131.6 1.7 %copy-start = (f32[4,128,128]{2,1,0:T(8,128)S(1)}, f32[4,128,128]{2,1,0:T(8,128)}, u32[]{:S(2)}) copy-start(f32[4,128,128]{2,1,0:T(8,128)} %get-tuple-element.5) | copy-start | bytes 786436

commit v5 on v4

--- a/solution.py
+++ b/solution.py
@@ -133,9 +133,11 @@
             l_send.at[n, d - 1], l_recv.at[n, d - 1], layer, t,
         )
 
-    def spread_start(n):
-        for d in range(1, nsplit):
+    def spread_start(n, distances=None):
+        for d in range(1, nsplit) if distances is None else distances:
             spread(n, d).start()
+        if distances is not None and 1 not in distances:
+            return
         for k in range(planes):
             lines[n, k, lines_of(s), :] = (dirb, imb, aimb, arb)[n][k, :, lanes(s)]
 
@@ -292,7 +294,7 @@
         return pl.ds(q * cb, cb)
 
     def shared(step):
-        return (0, width) if step == 1 else (nx // 2, width // 2)
+        return (0, width) if step == 1 else (nx - nx // 4, width // 4)
 
     def hand_share(way, step):
         base, size = shared(step)
@@ -303,7 +305,7 @@
         )
 
     def hand_whole(way, step):
-        part = pl.ds(0, nx // 2)
+        part = pl.ds(0, nx - nx // 4)
         return remote(
             xf.at[way, part, :], mbuf.at[step, part, :],
             x_send.at[way, 1], x_recv.at[step, 1], row_layer(hosts[way]), s,
@@ -349,43 +351,8 @@
             at = step if way == 0 else npos - 1 - step
             pl.when(pos == at)(functools.partial(do, step))
 
-    def host_prepare(way):
+    def row_vector(way):
         own = pall if way == 0 else qall
-        store_pair(own, xf[way])
-        order = (1, 0, 2)
-        for step in order:
-            hand_share(way, step).wait_recv()
-            ring(step, 0).start()
-            ring(step, 1).start()
-        for step in order:
-            ring(step, 0).wait_recv()
-            ring(step, 2).start()
-            ring(step, 1).wait_recv()
-            ring(step, 3).start()
-        upper, lower = pl.ds(0, nx // 2), pl.ds(nx // 2, nx // 2)
-        for step in order:
-            ring(step, 2).wait_recv()
-            ring(step, 3).wait_recv()
-            if step == 1:
-                store_pair(xpair.at[1], mbuf[1])
-            if step == 0:
-                pf[lower, :] = mm_ref(mbuf[0, lower, :], xpair.at[1])
-            if step == 2:
-                pin[lower, :] = mm_ref(mbuf[2, lower, :], own)
-        hand_whole(way, 0).wait_recv()
-        pf[upper, :] = mm_ref(mbuf[0, upper, :], xpair.at[1])
-        hand_whole(way, 2).wait_recv()
-        pin[upper, :] = mm_ref(mbuf[2, upper, :], own)
-        store_pair(xrow, pin[...])
-        pf[...] = mm_ref(pf[...], xrow)
-        store_pair(xrow, pf[...])
-        for step in (0, 2):
-            store_pair(xpair.at[step], mbuf[step])
-
-    def host_chain(way):
-        own = pall if way == 0 else qall
-        starts = line == 0 if way == 0 else line == nline - 1
-        ends = line == nline - 1 if way == 0 else line == 0
         for step in range(npos - 1):
             hand_vector(way, step).wait_recv()
         total = vbuf[0]
@@ -393,15 +360,70 @@
             total = vbuf[step] + mm_ref(total, xpair.at[step])
         zout[...] = vown[way] + mm_ref(total, own)
 
+    def line_starts(way):
+        return line == 0 if way == 0 else line == nline - 1
+
+    def line_ends(way):
+        return line == nline - 1 if way == 0 else line == 0
+
+    def send_first(way):
+        row_vector(way)
+        if nline > 1:
+            for q in range(nchunk):
+                hand_on(way, q).start()
+
+    def host_prepare(way, meanwhile):
+        own = pall if way == 0 else qall
+        store_pair(own, xf[way])
+        order = (1, 2, 0)
+        for step in order:
+            hand_share(way, step).wait_recv()
+            ring(step, 0).start()
+            ring(step, 1).start()
+        meanwhile()
+        for step in order:
+            ring(step, 0).wait_recv()
+            ring(step, 2).start()
+            ring(step, 1).wait_recv()
+            ring(step, 3).start()
+        upper, lower = pl.ds(0, nx - nx // 4), pl.ds(nx - nx // 4, nx // 4)
+        for step in order:
+            ring(step, 2).wait_recv()
+            ring(step, 3).wait_recv()
+            if step == 1:
+                store_pair(xpair.at[1], mbuf[1])
+            if step == 2:
+                hand_whole(way, 2).wait_recv()
+                store_pair(xpair.at[2], mbuf[2])
+        if way == 0:
+            pl.when(line_starts(way))(functools.partial(send_first, way))
+
+        @pl.when(jnp.logical_not(line_starts(way)))
+        def _():
+            store_pair(xrow, mm_pairs(xpair.at[2], own))
+            pf[lower, :] = mm_ref(mbuf[0, lower, :], xpair.at[1])
+
+        hand_whole(way, 0).wait_recv()
+
+        @pl.when(jnp.logical_not(line_starts(way)))
+        def _():
+            pf[upper, :] = mm_ref(mbuf[0, upper, :], xpair.at[1])
+            store_pair(xrow, mm_ref(pf[...], xrow))
+
+        store_pair(xpair.at[0], mbuf[0])
+
+    def host_chain(way):
+        starts, ends = line_starts(way), line_ends(way)
+
         @pl.when(starts)
         def _():
             inbuf[0] = jnp.zeros((yb, nx), F32)
-            if nline > 1:
-                for q in range(nchunk):
-                    hand_on(way, q).start()
+            if way == 1:
+                send_first(way)
 
         @pl.when(jnp.logical_not(starts))
         def _():
+            row_vector(way)
             for q in range(nchunk):
                 hand_on(way, q).wait_recv()
 
@@ -421,7 +443,7 @@
         (ain, bin_)[way][...] = state
 
     def host_finish(way):
-        ends = line == nline - 1 if way == 0 else line == 0
+        ends = line_ends(way)
         for step in range(npos - 1):
             hand_input(way, step).wait_send()
         for step in range(npos - 1):
@@ -499,56 +521,44 @@
         hand_wholes(1, lambda step: hand_whole(1, step).start())
         prepare()
 
-        @pl.when(pos == hosts[0])
-        def _():
-            give_r.wait_recv()
-            give_e0.wait_recv()
-            host_prepare(0)
-            host_chain(0)
-
-        @pl.when(pos != hosts[0])
-        def _():
-            response()
-            give_r.wait_recv()
-            store_pair(rpair, rin[...])
-            rin[...] = mm_ref(pf[...], rpair)
-            rf[...] = rf[...] + mm_ref(rin[...], qown)
-            store_pair(rpair, rf[...])
+        response()
+        give_r.wait_recv()
+        store_pair(rpair, rin[...])
+        rin[...] = mm_ref(pf[...], rpair)
+        rf[...] = rf[...] + mm_ref(rin[...], qown)
+        store_pair(rpair, rf[...])
+
+        def still():
             down_sweep(jnp.zeros((yb, nx), F32))
             up_partial(ezero)
             give_e0.wait_recv()
             ezero[...] = ezero[...] + mm_ref(ein0[...], qown)
 
+        @pl.when(pos == hosts[0])
+        def _():
+            host_prepare(0, still)
+            host_chain(0)
+
         @pl.when(pos == hosts[1])
         def _():
-            host_prepare(1)
+            host_prepare(1, still)
+
+        @pl.when(jnp.logical_and(pos != hosts[0], pos != hosts[1]))
+        def _():
+            still()
 
         for_step(0, lambda step: hand_input(0, step).wait_recv())
-
-        @pl.when(pos != hosts[0])
-        def _():
-            vown[1] = ezero[...] + mm_ref(ain[...], rpair)
-            for_step(1, lambda step: hand_vector(1, step).start())
-
+        vown[1] = ezero[...] + mm_ref(ain[...], rpair)
+        for_step(1, lambda step: hand_vector(1, step).start())
         amid[...] = cvec[...] + mm_ref(ain[...], pown)
         give_a.start()
         down_sweep(ain[...])
 
-        @pl.when(pos == hosts[0])
-        def _():
-            up_partial(evec)
-            give_e.wait_recv()
-            vown[1] = evec[...] + mm_ref(ein[...], qown)
-            hand_vector(1, 0).start()
-
         @pl.when(pos == hosts[1])
         def _():
             host_chain(1)
 
-        @pl.when(pos != hosts[0])
-        def _():
-            give_e.wait_recv()
-
+        give_e.wait_recv()
         for_step(1, lambda step: hand_input(1, step).wait_recv())
         give_b.start()
         up_sweep(ein[...] + mm_ref(bin_[...], q1))
@@ -566,10 +576,9 @@
     halo_wait(1)
     apply_operator(1, imb)
     halo_start(2)
-    spread_start(1)
+    spread_start(1, (1, nsplit - 1))
     halo_wait(2)
     apply_operator(2, aimb)
-    spread_start(2)
     put_sum(3, cols, imb)
     put_sum(4, arb, imb)
     put_sum(5, aimb, cols)
@@ -594,9 +603,15 @@
             2 * at + core, s,
         )
 
-    group[place] = part[...]
+    diagonal = lax.broadcasted_iota(jnp.int32, (nrow, width), 0) == lax.broadcasted_iota(
+        jnp.int32, (nrow, width), 1
+    )
+    sums = jnp.where(diagonal, jnp.sum(part[...], axis=1, keepdims=True), 0.0)
+    group[place] = jnp.sum(sums, axis=0, keepdims=True)
     for d in range(1, count):
         near(d).start()
+    spread_start(1, range(2, nsplit - 1))
+    spread_start(2)
     for n in (3, 0):
         spread_finish(n)
     for d in range(1, count):
@@ -614,8 +629,7 @@
     total = whole[0]
     for i in range(1, nchip):
         total = total + whole[i]
-    sums = jnp.sum(total, axis=1, keepdims=True)
-    rr, ar, aa, ri, ai, br, bi, ab, bb = [sums[i : i + 1, :] for i in range(9)]
+    rr, ar, aa, ri, ai, br, bi, ab, bb = [total[:, i : i + 1] for i in range(9)]
     alpha = rr / ri
     cross = ar - alpha * (ai + br) + alpha * alpha * bi
     own = aa - 2.0 * alpha * ab + alpha * alpha * bb
@@ -683,8 +697,8 @@
             pltpu.VMEM((4, planes, ysize, width), F32),
             pltpu.VMEM((4, planes, width, ysize), F32),
             pltpu.VMEM((nrow, width), F32),
-            pltpu.VMEM((2 * nsplit, nrow, width), F32),
-            pltpu.VMEM((nchip, nrow, width), F32),
+            pltpu.VMEM((2 * nsplit, 1, width), F32),
+            pltpu.VMEM((nchip, 1, width), F32),
             dma((2, nsplit - 1)), dma((2, nsplit - 1)),
             dma((4, planes)), dma((4, planes)),
             dma((9,)), dma((9,)),

time: 135 us -> 127 us (0.941)
  Pallas kernels: 131 us -> 123 us
    pallas_call x1, Pallas kernels: 131 us -> 123 us  [per_device(): pl.pallas_call(functools.partial(sweep_kernel, nlayer, nsplit, nchunk, nr...]
where the time goes in v5:
time: 127 us; the launch traced here: 126 us
  Pallas kernels  123 us (97%)
  local copies, waits for them, and re-layouts  2.42 us (2%)
    pallas_call x1, Pallas kernels, per_device(): pl.pallas_call(functools.partial(sweep_kernel, nlayer, nsplit, nchunk, nr...  123 us

profile of v5, /device:TPU:0, one launch (start us, length us, event | category | flops | bytes accessed | tf_op | source)
XLA Modules:
  0.0 126.4 jit_solution(1114732398359943330)
XLA Ops:
  0.6 123.3 %sweeps.1 = (f32[4,128,128]{2,1,0:T(8,128)}, f32[4,128,128]{2,1,0:T(8,128)}) custom-call(f32[4,128,128]{2,1,0:T(8,128)} %rhs_ref.1, f32[4,128,128]{2,1,0:T(8,128)} %diag_ref.1, f32[4,512,128]{2,1,0:T(8,128)} %inv_ref.1), custom_call_target="tpu_custom_call" | custom-call | tf_op jit(solution)/shard_map/sweeps/pallas_call | solution.py:677
  123.9 0.0 copy-start
  123.9 1.7 %copy.7 = f32[4,128,128]{2,1,0:T(8,128)} copy(f32[4,128,128]{2,1,0:T(8,128)} %get-tuple-element.4) | data formatting | bytes 524288
  125.6 0.0 copy-done
  125.7 0.7 copy.8
Async XLA Ops:
  123.9 1.7 %copy-start = (f32[4,128,128]{2,1,0:T(8,128)S(1)}, f32[4,128,128]{2,1,0:T(8,128)}, u32[]{:S(2)}) copy-start(f32[4,128,128]{2,1,0:T(8,128)} %get-tuple-element.5) | copy-start | bytes 786436

commit v6 on v5

--- a/solution.py
+++ b/solution.py
@@ -204,7 +204,6 @@
             regroup(1, d).wait_recv()
         halo_wait(0)
         apply_operator(0, arb)
-        spread_start(3)
         put_sum(0, cols, cols)
         put_sum(1, arb, cols)
         put_sum(2, arb, arb)
@@ -367,10 +366,8 @@
         return line == nline - 1 if way == 0 else line == 0
 
     def send_first(way):
-        row_vector(way)
-        if nline > 1:
-            for q in range(nchunk):
-                hand_on(way, q).start()
+        for q in range(nchunk):
+            hand_on(way, q).start()
 
     def host_prepare(way, meanwhile):
         own = pall if way == 0 else qall
@@ -386,44 +383,56 @@
             ring(step, 2).start()
             ring(step, 1).wait_recv()
             ring(step, 3).start()
+        starts = line_starts(way)
         upper, lower = pl.ds(0, nx - nx // 4), pl.ds(nx - nx // 4, nx // 4)
-        for step in order:
+
+        def passed(step):
             ring(step, 2).wait_recv()
             ring(step, 3).wait_recv()
-            if step == 1:
-                store_pair(xpair.at[1], mbuf[1])
-            if step == 2:
-                hand_whole(way, 2).wait_recv()
-                store_pair(xpair.at[2], mbuf[2])
+
+        def ahead_of_rest(part):
+            pin[part, :] = mm_ref(mbuf[2, part, :], own)
+
+        hand_whole(way, 2).wait_recv()
+        pl.when(jnp.logical_not(starts))(functools.partial(ahead_of_rest, upper))
+        passed(1)
+        store_pair(xpair.at[1], mbuf[1])
+        passed(2)
+        store_pair(xpair.at[2], mbuf[2])
         if way == 0:
-            pl.when(line_starts(way))(functools.partial(send_first, way))
-
-        @pl.when(jnp.logical_not(line_starts(way)))
-        def _():
-            store_pair(xrow, mm_pairs(xpair.at[2], own))
+            row_vector(way)
+            if nline > 1:
+                pl.when(starts)(functools.partial(send_first, way))
+        hand_whole(way, 0).wait_recv()
+
+        @pl.when(jnp.logical_not(starts))
+        def _():
+            pf[upper, :] = mm_ref(mbuf[0, upper, :], xpair.at[1])
+            ahead_of_rest(lower)
+            store_pair(xrow, pin[...])
+
+        passed(0)
+
+        @pl.when(jnp.logical_not(starts))
+        def _():
             pf[lower, :] = mm_ref(mbuf[0, lower, :], xpair.at[1])
-
-        hand_whole(way, 0).wait_recv()
-
-        @pl.when(jnp.logical_not(line_starts(way)))
-        def _():
-            pf[upper, :] = mm_ref(mbuf[0, upper, :], xpair.at[1])
             store_pair(xrow, mm_ref(pf[...], xrow))
 
         store_pair(xpair.at[0], mbuf[0])
 
     def host_chain(way):
         starts, ends = line_starts(way), line_ends(way)
+        if way == 1:
+            row_vector(way)
 
         @pl.when(starts)
         def _():
             inbuf[0] = jnp.zeros((yb, nx), F32)
-            if way == 1:
+            if way == 1 and nline > 1:
                 send_first(way)
 
         @pl.when(jnp.logical_not(starts))
         def _():
-            row_vector(way)
             for q in range(nchunk):
                 hand_on(way, q).wait_recv()
 
@@ -459,8 +468,7 @@
     def _():
         give_c.start()
         give_p.start()
-
-    absorb_up(planes - 1)
+        absorb_up(planes - 1)
 
     def down_sweep(state):
         for k in range(planes):
@@ -497,6 +505,7 @@
         down_sweep(ain[...])
         up_partial(evec)
         give_e.start()
+        spread_start(3)
         give_b.wait_recv()
         up_sweep(bcore[...])
         for give in (give_c, give_p, give_q, give_r, give_e0, give_e):
@@ -513,6 +522,7 @@
         for_step(0, lambda step: hand_vector(0, step).start())
         xf[0] = mm_pairs(pown, pall)
         for_step(0, lambda step: hand_share(0, step).start())
+        absorb_up(planes - 1)
         give_q.wait_recv()
         store_pair(q1, qin[...])
         xf[1] = mm_pairs(q1, qown)
@@ -522,13 +532,13 @@
         prepare()
 
         response()
-        give_r.wait_recv()
-        store_pair(rpair, rin[...])
-        rin[...] = mm_ref(pf[...], rpair)
-        rf[...] = rf[...] + mm_ref(rin[...], qown)
-        store_pair(rpair, rf[...])
 
         def still():
+            give_r.wait_recv()
+            store_pair(rpair, rin[...])
+            rin[...] = mm_pairs(pown, rpair)
+            rf[...] = rf[...] + mm_ref(rin[...], qown)
+            store_pair(rpair, rf[...])
             down_sweep(jnp.zeros((yb, nx), F32))
             up_partial(ezero)
             give_e0.wait_recv()
@@ -552,6 +562,7 @@
         for_step(1, lambda step: hand_vector(1, step).start())
         amid[...] = cvec[...] + mm_ref(ain[...], pown)
         give_a.start()
+        spread_start(3)
         down_sweep(ain[...])
 
         @pl.when(pos == hosts[1])
@@ -710,7 +721,7 @@
             dma((nchip - 1,)), dma((nchip - 1,)),
         ],
         compiler_params=pltpu.CompilerParams(
-            collective_id=0, has_side_effects=True, vmem_limit_bytes=56 * 1024 * 1024
+            collective_id=0, has_side_effects=True, vmem_limit_bytes=50 * 1024 * 1024
         ),
         name="sweeps",
     )(right_side, diagonal, inverses)

time: 127 us -> 126 us (level)
  Pallas kernels: 123 us -> 120 us
  local copies, waits for them, and re-layouts: 2.42 us -> 4.52 us
    pallas_call x1, Pallas kernels: 123 us -> 120 us  [per_device(): pl.pallas_call(functools.partial(sweep_kernel, nlayer, nsplit, nchunk, nr...]
    unnamed x4 -> x8, local copies, waits for them, and re-layouts: 2.42 us -> 4.52 us
where the time goes in v6:
time: 126 us; the launch traced here: 125 us
  Pallas kernels  120 us (95%)
  local copies, waits for them, and re-layouts  4.52 us (4%)
    pallas_call x1, Pallas kernels, per_device(): pl.pallas_call(functools.partial(sweep_kernel, nlayer, nsplit, nchunk, nr...  120 us
    unnamed x8, local copies, waits for them, and re-layouts  4.52 us

profile of v6, /device:TPU:0, one launch (start us, length us, event | category | flops | bytes accessed | tf_op | source)
XLA Modules:
  0.0 125.3 jit_solution(10169749444323071429)
XLA Ops:
  0.6 0.0 copy-start
  0.6 1.2 copy-done
  1.9 0.0 copy-start.1
  1.9 0.9 copy-done.1
  2.8 0.0 copy-start.2
  2.8 0.9 copy-done.2
  3.8 120.1 %sweeps.1 = (f32[4,128,128]{2,1,0:T(8,128)S(1)}, f32[4,128,128]{2,1,0:T(8,128)S(1)}) custom-call(f32[4,128,128]{2,1,0:T(8,128)S(1)} %copy-done.1, f32[4,128,128]{2,1,0:T(8,128)S(1)} %copy-done.2, f32[4,512,128]{2,1,0:T(8,128)S(1)} %copy-done), custom_call_target="tpu_custom_call" | custom-call | tf_op jit(solution)/shard_map/sweeps/pallas_call | solution.py:688
  123.9 0.7 copy.7
  124.6 0.7 copy.8
Async XLA Ops:
  0.6 1.2 copy-start
  1.9 0.9 copy-start.1
  2.8 0.9 copy-start.2

commit v7 on v6

--- a/solution.py
+++ b/solution.py
@@ -44,19 +44,20 @@
 
 def sweep_kernel(
     nlayer, nsplit, nchunk, nrow,
-    rhs_ref, diag_ref, inv_ref, sol_ref, res_ref,
+    rhs_in, diag_in, inv_in, sol_ref, res_ref,
     gbuf, mats, rsend, dsend, cols, dcols, low, dirb, imb, aimb, arb,
     pf, qf, pown, qown, pall, qall, q1, pin, qin,
     cvec, cin, ain, amid, evec, ein, bin_, bcore, zin, zout,
     xf, mbuf, xpair, xrow, vown, vbuf, inbuf,
     prefix, rf, rin, rpair, azero, ezero, ein0,
     zlow, zhigh, ylow, yhigh, edges, lines, flat, part, group, whole,
+    rhs_ref, diag_ref, inv_ref, in_sem,
     rs_send, rs_recv, g_send, g_recv, c_send, c_recv,
     x_send, x_recv, v_send, v_recv, i_send, i_recv, z_send, z_recv, y_send, y_recv,
     h_send, h_recv, l_send, l_recv, n_send, n_recv, w_send, w_recv,
 ):
-    planes, nx, width = inv_ref.shape
-    ysize = rhs_ref.shape[2]
+    planes, nx, width = inv_in.shape
+    ysize = rhs_in.shape[2]
     yb = ysize // nsplit
     cb = yb // nchunk
     half = width // 2
@@ -81,6 +82,14 @@
     def lines_of(t):
         return pl.ds(pl.multiple_of(t * yb, yb), yb)
 
+    loads = [
+        pltpu.make_async_copy(src, dst, in_sem.at[i])
+        for i, (src, dst) in enumerate(
+            ((inv_in, inv_ref), (rhs_in, rhs_ref), (diag_in, diag_ref))
+        )
+    ]
+    for load in loads:
+        load.start()
     for empty in (zlow, zhigh, ylow, yhigh, edges, part):
         empty[...] = jnp.zeros_like(empty)
 
@@ -102,9 +111,13 @@
     def _():
         greet(side, s)
 
+    loads[0].wait()
     for k in range(planes):
         gbuf[k, rows(s, 0, width), :] = inv_ref[k].T
-    for source, sent, mine in ((rhs_ref, rsend, cols), (diag_ref, dsend, dcols)):
+    for i, (source, sent, mine) in enumerate(
+        ((rhs_ref, rsend, cols), (diag_ref, dsend, dcols))
+    ):
+        loads[i + 1].wait()
         for k in range(planes):
             sent[k] = source[k].T
         for k in range(planes):
@@ -258,15 +271,18 @@
             qown[0] = high
             qown[1] = lowpart
         else:
-            cvec[...] = mm(cols[k] + cvec[...], high, lowpart)
             prefix[k - 1] = pf[...]
             pf[...] = mm(pf[...], high, lowpart)
+            if k == planes - 1:
+                pl.when(core == 1)(lambda: give_p.start())
+            cvec[...] = mm(cols[k] + cvec[...], high, lowpart)
 
     def absorb_up(k):
         if k > 0:
             qf[...] = mm(gbuf[k], qown[0], qown[1])
             store_pair(qown, qf[...])
 
+    give_p = remote(pf, pin, c_send.at[0], c_recv.at[0], other, s)
     for k in range(planes):
         relay(k)
         if k > 0:
@@ -274,7 +290,6 @@
             absorb_up(k - 1)
     absorb(planes - 1)
 
-    give_p = remote(pf, pin, c_send.at[0], c_recv.at[0], other, s)
     give_q = remote(qf, qin, c_send.at[1], c_recv.at[1], other, s)
     give_c = remote(cvec, cin, c_send.at[2], c_recv.at[2], other, s)
     give_a = remote(amid, ain, c_send.at[3], c_recv.at[3], other, s)
@@ -467,7 +482,6 @@
     @pl.when(core == 1)
     def _():
         give_c.start()
-        give_p.start()
         absorb_up(planes - 1)
 
     def down_sweep(state):
@@ -515,13 +529,13 @@
     def _():
         give_a0.start()
         store_pair(pown, pf[...])
-        give_c.wait_recv()
         give_p.wait_recv()
         store_pair(pall, pin[...])
+        xf[0] = mm_pairs(pown, pall)
+        for_step(0, lambda step: hand_share(0, step).start())
+        give_c.wait_recv()
         vown[0] = mm_ref(cvec[...], pall) + cin[...]
         for_step(0, lambda step: hand_vector(0, step).start())
-        xf[0] = mm_pairs(pown, pall)
-        for_step(0, lambda step: hand_share(0, step).start())
         absorb_up(planes - 1)
         give_q.wait_recv()
         store_pair(q1, qin[...])
@@ -688,7 +702,7 @@
     return pl.pallas_call(
         functools.partial(sweep_kernel, nlayer, nsplit, nchunk, nrow),
         out_shape=(shape, shape),
-        in_specs=[vmem] * 3,
+        in_specs=[pl.BlockSpec(memory_space=pltpu.HBM)] * 3,
         out_specs=(vmem, vmem),
         scratch_shapes=[
             pltpu.VMEM((planes, nx, nx), F32),
@@ -710,6 +724,8 @@
             pltpu.VMEM((nrow, width), F32),
             pltpu.VMEM((2 * nsplit, 1, width), F32),
             pltpu.VMEM((nchip, 1, width), F32),
+            pltpu.VMEM((planes, width, ysize), F32), pltpu.VMEM((planes, width, ysize), F32),
+            pltpu.VMEM((planes, nx, width), F32), dma((3,)),
             dma((2, nsplit - 1)), dma((2, nsplit - 1)),
             dma((4, planes)), dma((4, planes)),
             dma((9,)), dma((9,)),
@@ -721,7 +737,7 @@
             dma((nchip - 1,)), dma((nchip - 1,)),
         ],
         compiler_params=pltpu.CompilerParams(
-            collective_id=0, has_side_effects=True, vmem_limit_bytes=50 * 1024 * 1024
+            collective_id=0, has_side_effects=True, vmem_limit_bytes=56 * 1024 * 1024
         ),
         name="sweeps",
     )(right_side, diagonal, inverses)

time: 126 us -> 124 us (0.984)
  local copies, waits for them, and re-layouts: 4.52 us -> 2.42 us
    unnamed x8 -> x4, local copies, waits for them, and re-layouts: 4.52 us -> 2.42 us
where the time goes in v7:
time: 124 us
  Pallas kernels  121 us (98%)
  local copies, waits for them, and re-layouts  2.42 us (2%)
    pallas_call x1, Pallas kernels, per_device(): pl.pallas_call(functools.partial(sweep_kernel, nlayer, nsplit, nchunk, nr...  121 us

profile of v7, /device:TPU:0, one launch (start us, length us, event | category | flops | bytes accessed | tf_op | source)
XLA Modules:
  0.0 123.7 jit_solution(14736561121569553838)
XLA Ops:
  0.6 120.6 %sweeps.1 = (f32[4,128,128]{2,1,0:T(8,128)}, f32[4,128,128]{2,1,0:T(8,128)}) custom-call(f32[4,128,128]{2,1,0:T(8,128)} %rhs_in.1, f32[4,128,128]{2,1,0:T(8,128)} %diag_in.1, f32[4,512,128]{2,1,0:T(8,128)} %inv_in.1), custom_call_target="tpu_custom_call" | custom-call | tf_op jit(solution)/shard_map/sweeps/pallas_call | solution.py:702
  121.2 0.0 copy-start
  121.3 1.7 %copy.7 = f32[4,128,128]{2,1,0:T(8,128)} copy(f32[4,128,128]{2,1,0:T(8,128)} %get-tuple-element.4) | data formatting | bytes 524288
  123.0 0.0 copy-done
  123.0 0.7 copy.8
Async XLA Ops:
  121.2 1.7 %copy-start = (f32[4,128,128]{2,1,0:T(8,128)S(1)}, f32[4,128,128]{2,1,0:T(8,128)}, u32[]{:S(2)}) copy-start(f32[4,128,128]{2,1,0:T(8,128)} %get-tuple-element.5) | copy-start | bytes 786436

commit v8 on v7

--- a/solution.py
+++ b/solution.py
@@ -310,13 +310,25 @@
     def shared(step):
         return (0, width) if step == 1 else (nx - nx // 4, width // 4)
 
-    def hand_share(way, step):
+    def hand_share(way, step, piece=0):
         base, size = shared(step)
-        part = pl.ds(pl.multiple_of(base + s * size, size), size)
+        length = size // 2 if step == 1 else size
+        part = pl.ds(pl.multiple_of(base + s * size + piece * length, length), length)
         return remote(
             xf.at[way, part, :], mbuf.at[step, part, :],
-            x_send.at[way, 0], x_recv.at[step, 0], row_layer(hosts[way]), s,
-        )
+            x_send.at[way, 2 * piece], x_recv.at[step, 2 * piece], row_layer(hosts[way]), s,
+        )
+
+    def pieces(step):
+        return (0, 1) if step == 1 else (0,)
+
+    def shares_start(way, step):
+        for piece in pieces(step):
+            hand_share(way, step, piece).start()
+
+    def shares_end(way, step):
+        for piece in pieces(step):
+            hand_share(way, step, piece).wait_send()
 
     def hand_whole(way, step):
         part = pl.ds(0, nx - nx // 4)
@@ -350,15 +362,21 @@
 
     def ring(step, i):
         base, size = shared(step)
+        h = size // 2
+        own = (s, 0, size)
         owner, start, length = (
-            (s, 0, size), (s, 0, size), (left, 0, size // 2), (right, size // 2, size // 2)
+            (s, 0, h) if step == 1 else own, (s, h, h) if step == 1 else own,
+            (left, 0, h), (right, h, h), (s, h, h), (s, 0, h),
         )[i]
-        rows_at = pl.multiple_of(base + owner * size + start, size // 2)
+        rows_at = pl.multiple_of(base + owner * size + start, h)
         part = mbuf.at[step, pl.ds(rows_at, length), :]
         return remote(
             part, part, y_send.at[step, i], y_recv.at[step, i], layer,
-            (right, left, right, left)[i],
-        )
+            (right, left, right, left, right, left)[i],
+        )
+
+    def ring_copies(step):
+        return range(6) if step == 1 else range(4)
 
     def for_step(way, do):
         for step in range(npos - 1):
@@ -391,19 +409,23 @@
         for step in order:
             hand_share(way, step).wait_recv()
             ring(step, 0).start()
+            if step == 1:
+                ring(step, 5).start()
+                hand_share(way, step, 1).wait_recv()
+                ring(step, 4).start()
             ring(step, 1).start()
-        meanwhile()
         for step in order:
             ring(step, 0).wait_recv()
             ring(step, 2).start()
             ring(step, 1).wait_recv()
             ring(step, 3).start()
+        meanwhile()
         starts = line_starts(way)
         upper, lower = pl.ds(0, nx - nx // 4), pl.ds(nx - nx // 4, nx // 4)
 
         def passed(step):
-            ring(step, 2).wait_recv()
-            ring(step, 3).wait_recv()
+            for i in ring_copies(step)[2:]:
+                ring(step, i).wait_recv()
 
         def ahead_of_rest(part):
             pin[part, :] = mm_ref(mbuf[2, part, :], own)
@@ -471,7 +493,7 @@
         for step in range(npos - 1):
             hand_input(way, step).wait_send()
         for step in range(npos - 1):
-            for i in range(4):
+            for i in ring_copies(step):
                 ring(step, i).wait_send()
 
         @pl.when(jnp.logical_not(ends))
@@ -532,7 +554,7 @@
         give_p.wait_recv()
         store_pair(pall, pin[...])
         xf[0] = mm_pairs(pown, pall)
-        for_step(0, lambda step: hand_share(0, step).start())
+        for_step(0, functools.partial(shares_start, 0))
         give_c.wait_recv()
         vown[0] = mm_ref(cvec[...], pall) + cin[...]
         for_step(0, lambda step: hand_vector(0, step).start())
@@ -540,7 +562,7 @@
         give_q.wait_recv()
         store_pair(q1, qin[...])
         xf[1] = mm_pairs(q1, qown)
-        for_step(1, lambda step: hand_share(1, step).start())
+        for_step(1, functools.partial(shares_start, 1))
         hand_wholes(0, lambda step: hand_whole(0, step).start())
         hand_wholes(1, lambda step: hand_whole(1, step).start())
         prepare()
@@ -592,7 +614,7 @@
         give_b.wait_send()
         for way in range(2):
             for_step(way, lambda step, way=way: hand_vector(way, step).wait_send())
-            for_step(way, lambda step, way=way: hand_share(way, step).wait_send())
+            for_step(way, functools.partial(shares_end, way))
             hand_wholes(way, lambda step, way=way: hand_whole(way, step).wait_send())
             pl.when(pos == hosts[way])(functools.partial(host_finish, way))
 
@@ -729,8 +751,8 @@
             dma((2, nsplit - 1)), dma((2, nsplit - 1)),
             dma((4, planes)), dma((4, planes)),
             dma((9,)), dma((9,)),
-            dma((2, 2)), dma((3, 2)), dma((2,)), dma((3,)), dma((3,)), dma((2,)),
-            dma((nchunk,)), dma((nchunk,)), dma((3, 4)), dma((3, 4)),
+            dma((2, 3)), dma((3, 3)), dma((2,)), dma((3,)), dma((3,)), dma((2,)),
+            dma((nchunk,)), dma((nchunk,)), dma((3, 6)), dma((3, 6)),
             dma((3, 4)), dma((3, 4)),
             dma((4, nsplit - 1)), dma((4, nsplit - 1)),
             dma((2 * nsplit - 1,)), dma((2 * nsplit - 1,)),

time: 124 us -> 123 us (level)
  no operation moved by 1% of the time
where the time goes in v8:
time: 123 us
  Pallas kernels  120 us (98%)
  local copies, waits for them, and re-layouts  2.42 us (2%)
    pallas_call x1, Pallas kernels, per_device(): pl.pallas_call(functools.partial(sweep_kernel, nlayer, nsplit, nchunk, nr...  120 us

profile of v8, /device:TPU:0, one launch (start us, length us, event | category | flops | bytes accessed | tf_op | source)
XLA Modules:
  0.0 123.2 jit_solution(651610391234596290)
XLA Ops:
  0.6 120.1 %sweeps.1 = (f32[4,128,128]{2,1,0:T(8,128)}, f32[4,128,128]{2,1,0:T(8,128)}) custom-call(f32[4,128,128]{2,1,0:T(8,128)} %rhs_in.1, f32[4,128,128]{2,1,0:T(8,128)} %diag_in.1, f32[4,512,128]{2,1,0:T(8,128)} %inv_in.1), custom_call_target="tpu_custom_call" | custom-call | tf_op jit(solution)/shard_map/sweeps/pallas_call | solution.py:724
  120.7 0.0 copy-start
  120.7 1.7 %copy.7 = f32[4,128,128]{2,1,0:T(8,128)} copy(f32[4,128,128]{2,1,0:T(8,128)} %get-tuple-element.4) | data formatting | bytes 524288
  122.5 0.0 copy-done
  122.5 0.7 copy.8
Async XLA Ops:
  120.7 1.7 %copy-start = (f32[4,128,128]{2,1,0:T(8,128)S(1)}, f32[4,128,128]{2,1,0:T(8,128)}, u32[]{:S(2)}) copy-start(f32[4,128,128]{2,1,0:T(8,128)} %get-tuple-element.5) | copy-start | bytes 786436

commit v9 on v8

--- a/solution.py
+++ b/solution.py
@@ -164,7 +164,8 @@
         values = (cols, dirb, imb)[n]
         src = (values.at[planes - 1], values.at[0], edges.at[n, 0], edges.at[n, 1])[i]
         dst = (zlow, zhigh, ylow, yhigh)[i].at[n]
-        l, t = ((layer + 1, s), (layer - 1, s), (layer, s + 1), (layer, s - 1))[i]
+        up, down = lax.rem(layer + 1, nlayer), lax.rem(layer + nlayer - 1, nlayer)
+        l, t = ((up, s), (down, s), (layer, right), (layer, left))[i]
         return remote(src, dst, h_send.at[n, i], h_recv.at[n, i], l, t)
 
     to_high, to_low = layer < nlayer - 1, layer > 0
@@ -357,7 +358,7 @@
     def hand_on(way, q):
         return remote(
             zout.at[chunk(q), :], zin.at[chunk(q), :], z_send.at[q], z_recv.at[q],
-            layer + (2 - 4 * way) * npos, s,
+            lax.rem(layer + nlayer + (2 - 4 * way) * npos, nlayer), s,
         )
 
     def ring(step, i):

time: 123 us -> 123 us (level)
  no operation moved by 1% of the time
where the time goes in v9:
time: 123 us
  Pallas kernels  120 us (98%)
  local copies, waits for them, and re-layouts  2.42 us (2%)
    pallas_call x1, Pallas kernels, per_device(): pl.pallas_call(functools.partial(sweep_kernel, nlayer, nsplit, nchunk, nr...  120 us

profile of v9, /device:TPU:0, one launch (start us, length us, event | category | flops | bytes accessed | tf_op | source)
XLA Modules:
  0.0 123.2 jit_solution(14736633038383877774)
XLA Ops:
  0.6 120.1 %sweeps.1 = (f32[4,128,128]{2,1,0:T(8,128)}, f32[4,128,128]{2,1,0:T(8,128)}) custom-call(f32[4,128,128]{2,1,0:T(8,128)} %rhs_in.1, f32[4,128,128]{2,1,0:T(8,128)} %diag_in.1, f32[4,512,128]{2,1,0:T(8,128)} %inv_in.1), custom_call_target="tpu_custom_call" | custom-call | tf_op jit(solution)/shard_map/sweeps/pallas_call | solution.py:725
  120.7 0.0 copy-start
  120.7 1.7 %copy.7 = f32[4,128,128]{2,1,0:T(8,128)} copy(f32[4,128,128]{2,1,0:T(8,128)} %get-tuple-element.4) | data formatting | bytes 524288
  122.5 0.0 copy-done
  122.5 0.7 copy.8
Async XLA Ops:
  120.7 1.7 %copy-start = (f32[4,128,128]{2,1,0:T(8,128)S(1)}, f32[4,128,128]{2,1,0:T(8,128)}, u32[]{:S(2)}) copy-start(f32[4,128,128]{2,1,0:T(8,128)} %get-tuple-element.5) | copy-start | bytes 786436
